TPU v7x, 8 devices: a whole 2x2x1 slice. The times are simulated.
8 devices in a mesh: batch: 1 (over z), col: 2 (over y), row: 4 (over x, core).
Axes of the slice: x: 2, y: 2, z: 1, core: 2. Of those that a mesh axis runs over, the one named last changes fastest.
Arguments:
- x: bfloat16 [16, 32, 512, 32], P('batch', 'row', 'col')
- w_down_1: bfloat16 [3, 3, 32, 64], replicated
- b_down_1: float32 [64], replicated
- w_conv_1: bfloat16 [3, 3, 64, 64], replicated
- b_conv_1: float32 [64], replicated
- w_proj_1: bfloat16 [32, 64], replicated
- w_down_2: bfloat16 [3, 3, 64, 128], replicated
- b_down_2: float32 [128], replicated
- w_conv_2: bfloat16 [3, 3, 128, 128], replicated
- b_conv_2: float32 [128], replicated
- w_proj_2: bfloat16 [64, 128], replicated
- w_down_3: bfloat16 [3, 3, 128, 256], replicated
- b_down_3: float32 [256], replicated
- w_conv_3: bfloat16 [3, 3, 256, 256], replicated
- b_conv_3: float32 [256], replicated
- w_proj_3: bfloat16 [128, 256], replicated
Outputs:
- output: bfloat16 [16, 4, 64, 256], P('batch', 'row', 'col')
All inputs are finite; a program needn't handle non-finite values.
Results may differ from a plain program's by a relative error of at most 0.00239.
Values are sent between devices in bfloat16 or wider.
A program may use at most 1 GiB of HBM per device.

v0:
```python
import functools

import jax
import jax.numpy as jnp
from jax import lax
from jax.experimental import pallas as pl
from jax.experimental.pallas import tpu as pltpu
from jax.sharding import PartitionSpec as P

MESH = pl.DeviceIdType.MESH
BF = jnp.bfloat16
F32 = jnp.float32

L = 128
LL = 2 * L
H = L // 2
Q = L // 4
LO = slice(0, L)
HI = slice(L, LL)
IMG = 16
N = 5
PAD = 12
COLS = (140, 70, 35)
M = tuple(p // N for p in COLS)
MH = M[0] // 2
STEP = 132
TAPS = range(3)
MIB = 1024 * 1024

(X_TOP, X_COL, Y1_DOWN, Y1_UP, Z1_DOWN, Y2_DOWN, Y2_UP, Z2_DOWN, Y3_DOWN, Y3_UP, MESSAGES) = range(11)


def _dot(a, b):
    return jnp.dot(a, b, preferred_element_type=F32)


def _flat(v):
    return v.reshape(v.shape[0] * v.shape[1], v.shape[2])


def _roll(v, shift):
    return pltpu.roll(v, shift, v.ndim - 1)


def _lane(shape):
    return lax.broadcasted_iota(jnp.int32, shape, len(shape) - 1)


def _relu(v):
    return jnp.maximum(v, 0.0)


def _body(row_count, *refs):
    (x_hbm, wd1_h, bd1, wc1_h, bc1, wp1_h, wd2_h, bd2, wc2_h, bc2, wp2_h, wd3_h, bd3, wc3_h, bc3, wp3_h,
     out_ref,
     xv, xt, xtop, xh, fs, sdiag, rdiag, bias,
     wd1r, wc1r, wp1r, wd2r, wc2r, wp2r, wd3, wc3, wp3,
     wd1, wdh1, wc1, wch1, wpp1, wd2, wdh2, wc2, wch2, wpp2,
     part1, part2, part3, acc1, acc2, acc3, y1, y2, y3, z1, z2, zo,
     sy1d, sy1u, sz1, ry1d, ry1u, rz1,
     yh1, yh2, yt3, yb3, zh1, zh2,
     xsem, wsem, ssem, rsem) = refs

    row = lax.axis_index("row")
    col = lax.axis_index("col")
    outer, inner = col, 1 - col
    has_up = row > 0
    has_down = row < row_count - 1
    up = {"row": row - 1}
    down = {"row": row + 1}
    side = {"col": 1 - col}
    diag_down = {"row": row + 1, "col": 1 - col}
    diag_up = {"row": row - 1, "col": 1 - col}

    barrier = pltpu.get_barrier_semaphore()

    def greet(device):
        pl.semaphore_signal(barrier, inc=1, device_id=device, device_id_type=MESH)

    greet(side)

    @pl.when(has_up)
    def _():
        greet(up)
        greet(diag_up)

    @pl.when(has_down)
    def _():
        greet(down)
        greet(diag_down)

    def x_copy(h):
        return pltpu.make_async_copy(x_hbm.at[:, :, :, pl.ds(pl.multiple_of(h * L, L), L)], xv.at[h], xsem.at[h])

    w_copies = [pltpu.make_async_copy(s, d, wsem.at[i]) for i, (s, d) in enumerate(
        ((wd1_h, wd1r), (wc1_h, wc1r), (wp1_h, wp1r), (wd2_h, wd2r), (wc2_h, wc2r), (wp2_h, wp2r),
         (wd3_h, wd3), (wc3_h, wc3), (wp3_h, wp3)))]
    w_copies[0].start()
    x_copy(inner).start()
    x_copy(outer).start()
    for c in w_copies[1:]:
        c.start()

    def remote(src, dst, msg, k, dev):
        return pltpu.make_async_remote_copy(src_ref=src, dst_ref=dst, send_sem=ssem.at[msg, k], recv_sem=rsem.at[msg, k],
                                            device_id=dev, device_id_type=MESH)

    def m_xtop(h):
        return remote(x_hbm.at[:, 7, :, pl.ds(pl.multiple_of(h * L, L), L)], xtop.at[h], X_TOP, h, down)

    def m_diag():
        return remote(sdiag, rdiag, X_TOP, 2, diag_down)

    own_edge = 1 + (L - PAD) * inner + PAD * col
    far_edge = 1 + L * col

    def m_xcol():
        return remote(xt.at[pl.ds(own_edge, PAD)], xt.at[pl.ds(far_edge, PAD)], X_COL, 0, side)

    def plain(src, dst, msg, dev, first, size, src_lanes=None, dst_lanes=None):
        def make(k):
            s = pl.ds(first + order(k) * size, size)
            return remote(src.at[s] if src_lanes is None else src.at[s, :, src_lanes],
                          dst.at[s] if dst_lanes is None else dst.at[s, :, dst_lanes], msg, k, dev)
        return make

    def order(k):
        return k + col * (N - 1 - 2 * k)

    lanes_lo, lanes_hi = pl.ds(0, L), pl.ds(L, L)
    m_y1d = plain(sy1d, ry1d, Y1_DOWN, down, 0, MH)
    m_y1u = plain(sy1u, ry1u, Y1_UP, up, 0, MH)
    m_z1 = plain(sz1, rz1, Z1_DOWN, down, 0, MH)
    m_y2d = plain(y2, yh2, Y2_DOWN, down, 1, M[1], lanes_hi, lanes_lo)
    m_y2u = plain(y2, yh2, Y2_UP, up, 1, M[1], lanes_lo, lanes_hi)
    m_y3d = plain(y3, yt3, Y3_DOWN, down, 1, M[2])
    m_y3u = plain(y3, yb3, Y3_UP, up, 1, M[2])

    def m_z2(k):
        s = pl.ds(1 + order(k) * M[2], M[2])
        return remote(z2.at[s, :, :, lanes_hi], zh2.at[s], Z2_DOWN, k, down)

    def send(downs, ups, k):
        if downs:
            @pl.when(has_down)
            def _():
                for m in downs:
                    m(k).start()
        if ups:
            @pl.when(has_up)
            def _():
                for m in ups:
                    m(k).start()

    def recv(downs, ups, k):
        if downs:
            @pl.when(has_up)
            def _():
                for m in downs:
                    m(k).wait_recv()
        if ups:
            @pl.when(has_down)
            def _():
                for m in ups:
                    m(k).wait_recv()

    for ref in (xt, xh, z1, z2, zh1, zh2, y1, y2, y3, yh1, yh2, yt3, yb3):
        ref[0] = jnp.zeros(ref.shape[1:], BF)
    for ref in (y1, y2, y3, yh1, yh2, yt3, yb3):
        ref[ref.shape[0] - 1] = jnp.zeros(ref.shape[1:], BF)
    for i, (b, reps) in enumerate(((bd1, 4), (bc1, 4), (bd2, 2), (bc2, 2), (bd3, 1), (bc3, 1))):
        v = jnp.concatenate([b[...]] * reps, axis=-1)
        bias[i] = jnp.broadcast_to(v, (IMG, LL))

    neighbours = 1 + 2 * jnp.minimum(row, 1) + 2 * jnp.minimum(row_count - 1 - row, 1)
    pl.semaphore_wait(barrier, neighbours)

    send([m_xtop], [], outer)
    send([m_xtop], [], inner)

    @pl.when(jnp.logical_not(has_up))
    def _():
        for ref in (xtop, rdiag, ry1d, rz1, zh2, yt3):
            ref[...] = jnp.zeros(ref.shape, BF)
        yh2[:, :, LO] = jnp.zeros((yh2.shape[0], IMG, L), BF)

    @pl.when(jnp.logical_not(has_down))
    def _():
        for ref in (ry1u, yb3):
            ref[...] = jnp.zeros(ref.shape, BF)
        yh2[:, :, HI] = jnp.zeros((yh2.shape[0], IMG, L), BF)

    def toeplitz(dst, rows_in, rows_out, shape, piece):
        for r in range(rows_in):
            parts = []
            for i in range(rows_out):
                v = piece(r, i)
                parts.append(jnp.zeros(shape, BF) if v is None else v)
            dst[r * shape[0]:(r + 1) * shape[0], :] = jnp.concatenate(parts, axis=1)

    def tap_of(w, kw, stride):
        def piece(r, i):
            kh = r - stride * i + 1
            return w[kh, kw] if kh in TAPS else None
        return piece

    w_copies[0].wait()
    s_d1, s_c1 = wd1r.shape[2:], wc1r.shape[2:]
    for kw in TAPS:
        toeplitz(wd1.at[kw], 8, 4, s_d1, tap_of(wd1r, kw, 2))
    toeplitz(wdh1, 4, 2, s_d1, lambda r, i: wd1r[0, r] if r in TAPS and i == 0 else None)

    def transpose_half(h):
        for n in range(IMG):
            for g in range(2):
                block = xv[h, n, 4 * g:4 * g + 4].reshape(L, L)
                fs[g, n * STEP:n * STEP + L, :] = block.T.astype(F32)
        base = 1 + PAD * col + H * h

        @pl.loop(0, H, unroll=8)
        def _(p):
            for e in range(2):
                v = [fs[g, pl.ds(2 * p + e, IMG, stride=STEP), :] for g in range(2)]
                xt[base + p, e] = jnp.concatenate(v, axis=-1).astype(BF)

    def transpose_top(h):
        for n in range(IMG):
            block = jnp.concatenate([xtop[h, n]] * 4, axis=0)
            fs[0, n * STEP:n * STEP + L, :] = block.T.astype(F32)
        base = 1 + PAD * col + H * h

        @pl.loop(0, H, unroll=8)
        def _(p):
            for e in range(2):
                xh[base + p, e] = fs[0, pl.ds(2 * p + e, IMG, stride=STEP), :].astype(BF)

    quads = (PAD // 2, 4, IMG, L)

    def pack_diag():
        v = xt[pl.ds(own_edge, PAD), :, :, HI].astype(F32).reshape(quads)
        ln = _lane((quads[0], IMG, L))
        r = v[:, 3]
        for q in TAPS:
            r = jnp.where((ln >= q * Q) & (ln < (q + 1) * Q), _roll(v[:, q], (q + 1) * Q), r)
        sdiag[...] = r.astype(BF)

    def unpack_diag():
        v = rdiag[...].astype(F32)
        ln = _lane(v.shape)
        out = []
        for q in range(4):
            r = jnp.where((ln >= q * Q) & (ln < (q + 1) * Q), v, 0.0)
            r = r + _roll(r, Q)
            out.append(r + _roll(r, H))
        u = jnp.stack(out, axis=1).astype(BF)
        xh[pl.ds(1 + L * (1 - col), PAD)] = u.reshape(PAD, 2, IMG, L)

    x_copy(inner).wait()
    transpose_half(inner)
    m_xcol().start()
    pack_diag()

    @pl.when(has_down)
    def _():
        m_diag().start()

    x_copy(outer).wait()
    transpose_half(outer)

    def taps(ref, j0, m):
        return [_flat(ref[pl.ds(j0 + t, m)]) for t in TAPS]

    def pair_taps(ref, j0, m):
        return [_flat(ref[pl.ds(j0, m), 1]), _flat(ref[pl.ds(j0 + 1, m), 0]), _flat(ref[pl.ds(j0 + 1, m), 1])]

    def sum_dots(lhs, w):
        v = _dot(lhs[0], w(0))
        for t in TAPS[1:]:
            v = v + _dot(lhs[t], w(t))
        return v

    def tiles(v, m):
        return v.reshape(m, IMG, v.shape[-1])

    low = _lane((MH, IMG, L)) < H

    def pack(a, b):
        return jnp.where(low, a, b).astype(BF)

    m1, m2, m3 = M

    def down1(k):
        j0 = order(k) * m1
        v = tiles(sum_dots(pair_taps(xt, j0, m1), lambda t: wd1[t]), m1)
        part1[pl.ds(j0, m1)] = v[:, :, LO]
        hi = _relu(v[:, :, HI] + bias[0, :, HI])
        y1[pl.ds(1 + j0, m1), :, HI] = hi.astype(BF)
        sy1d[pl.ds(order(k) * MH, MH)] = pack(_roll(hi[:MH], H), hi[MH:])

    def top1(k):
        j0 = order(k) * m1
        a, b, c = pair_taps(xh, j0, m1)
        ln = _lane(a.shape)
        v = tiles(_dot(jnp.where(ln < Q, a, jnp.where(ln < H, b, c)), wdh1[...]), m1)
        lo = _relu(v + part1[pl.ds(j0, m1)] + bias[0, :, LO])
        y1[pl.ds(1 + j0, m1), :, LO] = lo.astype(BF)
        sy1u[pl.ds(order(k) * MH, MH)] = pack(lo[:MH], _roll(lo[MH:], H))

    def conv1(k):
        j0 = order(k) * m1
        v = sum_dots(taps(y1, j0, m1), lambda t: wc1[t]) + _dot(_flat(xt[pl.ds(j0 + 1, m1), 0]), wpp1[...])
        acc1[pl.ds(j0, m1)] = tiles(v, m1) + bias[1]

    def unpack1(k):
        s = pl.ds(order(k) * MH, MH)
        t, b = ry1d[s].astype(F32), ry1u[s].astype(F32)
        yh1[pl.ds(1 + order(k) * m1, MH)] = pack(t, _roll(b, H))
        yh1[pl.ds(1 + order(k) * m1 + MH, MH)] = pack(_roll(t, H), b)

    def halo1(k):
        j0 = order(k) * m1
        v = tiles(sum_dots(taps(yh1, j0, m1), lambda t: wch1[t]), m1)
        v = _relu(v + acc1[pl.ds(j0, m1)])
        z1[pl.ds(1 + order(k) * MH, MH)] = v.astype(BF).reshape(MH, 2, IMG, LL)
        hi = v[:, :, HI]
        sz1[pl.ds(order(k) * MH, MH)] = pack(_roll(hi[:MH], H), hi[MH:])

    def down2(k):
        j0 = order(k) * m2
        v = tiles(sum_dots(pair_taps(z1, j0, m2), lambda t: wd2[t]), m2)
        part2[pl.ds(j0, m2)] = v[:, :, LO]
        y2[pl.ds(1 + j0, m2), :, HI] = _relu(v[:, :, HI] + bias[2, :, HI]).astype(BF)

    def unpack2(k):
        s = order(k) * MH
        half = MH // 2
        t = rz1[pl.ds(s, MH)].astype(F32)
        u = _roll(t, H)
        zh1[pl.ds(1 + s, half)] = pack(t, u).reshape(half, 2, IMG, L)
        zh1[pl.ds(1 + s + half, half)] = pack(u, t).reshape(half, 2, IMG, L)

    def top2(k):
        j0 = order(k) * m2
        a, b, c = pair_taps(zh1, j0, m2)
        t = jnp.concatenate([jnp.where(_lane(a.shape) < H, a, b), c], axis=-1)
        v = tiles(_dot(t, wdh2[...]), m2) + part2[pl.ds(j0, m2)]
        y2[pl.ds(1 + j0, m2), :, LO] = _relu(v + bias[2, :, LO]).astype(BF)

    def conv2(k):
        j0 = order(k) * m2
        v = sum_dots(taps(y2, j0, m2), lambda t: wc2[t]) + _dot(_flat(z1[pl.ds(j0 + 1, m2), 0]), wpp2[...])
        acc2[pl.ds(j0, m2)] = tiles(v, m2) + bias[3]

    def halo2(k):
        j0 = order(k) * m2
        v = tiles(sum_dots(taps(yh2, j0, m2), lambda t: wch2[t]), m2) + acc2[pl.ds(j0, m2)]
        z2[pl.ds(1 + order(k) * m3, m3)] = _relu(v).astype(BF).reshape(m3, 2, IMG, LL)

    def down3(k):
        j0 = order(k) * m3
        v = sum_dots(pair_taps(z2, j0, m3), lambda t: wd3[1:, t].reshape(LL, LL))
        part3[pl.ds(j0, m3)] = tiles(v, m3) + bias[4]

    def top3(k):
        j0 = order(k) * m3
        v = tiles(sum_dots(pair_taps(zh2, j0, m3), lambda t: wd3[0, t]), m3) + part3[pl.ds(j0, m3)]
        y3[pl.ds(1 + j0, m3)] = _relu(v).astype(BF)

    def conv3(k):
        j0 = order(k) * m3
        v = sum_dots(taps(y3, j0, m3), lambda t: wc3[1, t]) + _dot(_flat(z2[pl.ds(j0 + 1, m3), 0, :, LO]), wp3[...])
        acc3[pl.ds(j0, m3)] = tiles(v, m3) + bias[5]

    def halo3(k):
        j0 = order(k) * m3
        v = sum_dots(taps(yt3, j0, m3), lambda t: wc3[0, t]) + sum_dots(taps(yb3, j0, m3), lambda t: wc3[2, t])
        v = _relu(tiles(v, m3) + acc3[pl.ds(j0, m3)])
        r = pl.ds(pl.multiple_of(j0 * IMG, IMG), m3 * IMG)
        zo[0, r] = _flat(v[:, :, LO])
        zo[1, r] = _flat(v[:, :, HI])

    last = N - 1

    def wait_next(downs, ups, k):
        if k == 0:
            recv(downs, ups, 0)
        if k < last:
            recv(downs, ups, k + 1)

    for k in range(N - 1):
        down1(k)
        send([m_y1d], [], k)

    recv([m_xtop], [], outer)
    transpose_top(outer)
    for k in range(2):
        top1(k)
        send([], [m_y1u], k)

    for c in w_copies[1:]:
        c.wait()
    for kw in TAPS:
        toeplitz(wc1.at[kw], 4, 4, s_c1, tap_of(wc1r, kw, 1))
    toeplitz(wpp1, 8, 4, s_d1, lambda r, i: wp1r[...] if r == 2 * i else None)

    recv([m_xtop], [], inner)
    transpose_top(inner)
    for k in range(2, N - 1):
        conv1(k - 2)
        top1(k)
        send([], [m_y1u], k)

    for kw in TAPS:
        toeplitz(wch1.at[kw], 2, 4, s_c1, lambda r, i: wc1r[2 * r, kw] if i == 3 * r else None)
    m_xcol().wait_recv()
    conv1(2)
    down1(last)
    send([m_y1d], [], last)

    @pl.when(has_up)
    def _():
        m_diag().wait_recv()

    unpack_diag()
    top1(last)
    send([], [m_y1u], last)

    s_d2, s_c2 = wd2r.shape[2:], wc2r.shape[2:]
    for kw in TAPS:
        toeplitz(wd2.at[kw], 4, 2, s_d2, tap_of(wd2r, kw, 2))
        toeplitz(wc2.at[kw], 2, 2, s_c2, tap_of(wc2r, kw, 1))
        toeplitz(wch2.at[kw], 2, 2, s_c2, lambda r, i: wc2r[2 * r, kw] if i == r else None)
    toeplitz(wpp2, 4, 2, s_d2, lambda r, i: wp2r[...] if r == 2 * i else None)
    toeplitz(wdh2, 4, 1, s_d2, lambda r, i: wd2r[0, r] if r in TAPS else None)

    conv1(3)
    recv([m_y1d], [m_y1u], 0)
    unpack1(0)
    for k in range(N):
        if k < last:
            recv([m_y1d], [m_y1u], k + 1)
            unpack1(k + 1)
        if k == 0:
            conv1(last)
        if k >= 2:
            down2(k - 2)
        halo1(k)
        send([m_z1], [], k)
        if k >= 2:
            send([m_y2d], [], k - 2)

    recv([m_z1], [], 0)
    unpack2(0)
    for k in range(N):
        if k < last:
            recv([m_z1], [], k + 1)
            unpack2(k + 1)
        if k < 2:
            down2(k + 3)
        else:
            conv2(k - 2)
        top2(k)
        send([], [m_y2u], k)
        if k < 2:
            send([m_y2d], [], k + 3)

    for k in range(N):
        wait_next([m_y2d], [m_y2u], k)
        if k < 2:
            conv2(k + 3)
        else:
            down3(k - 2)
        halo2(k)
        send([m_z2], [], k)

    for k in range(N):
        wait_next([m_z2], [], k)
        if k < 2:
            down3(k + 3)
        else:
            conv3(k - 2)
        top3(k)
        send([m_y3d], [m_y3u], k)

    for k in range(N):
        wait_next([m_y3d], [m_y3u], k)
        if k < 2:
            conv3(k + 3)
        halo3(k)

    for n in range(IMG):
        v = [zo[g, pl.ds(PAD * 4 * col + n, out_ref.shape[2], stride=IMG), :] for g in range(2)]
        out_ref[n, 0] = jnp.concatenate(v, axis=-1).astype(BF)

    m_xcol().wait_send()

    @pl.when(has_down)
    def _():
        m_diag().wait_send()
        for h in range(2):
            m_xtop(h).wait_send()

        @pl.loop(0, N)
        def _(k):
            for m in (m_y1d, m_z1, m_y2d, m_z2, m_y3d):
                m(k).wait_send()

    @pl.when(has_up)
    def _():
        @pl.loop(0, N)
        def _(k):
            for m in (m_y1u, m_y2u, m_y3u):
                m(k).wait_send()


def solution(mesh):
    row_count = mesh.shape["row"]
    tile_spec = P("batch", "row", "col")
    c1, c2, c3 = COLS

    def vm(*shape, dtype=BF):
        return pltpu.VMEM(shape, dtype)

    def weights(cin, cout):
        return [vm(3, 3, cin, cout), vm(3, 3, cout, cout), vm(cin, cout)]

    packed = vm(c2, IMG, L)
    scratch = [
        vm(2, IMG, 8, Q, L), vm(c1 + 1, 2, IMG, LL), vm(2, IMG, Q, L), vm(c1 + 1, 2, IMG, L),
        vm(2, IMG * STEP, L, dtype=F32), vm(PAD // 2, IMG, L), vm(PAD // 2, IMG, L), vm(6, IMG, LL, dtype=F32),
        *weights(Q, H), *weights(H, L), *weights(L, LL),
        vm(3, LL, LL), vm(L, L), vm(3, LL, LL), vm(3, L, LL), vm(LL, LL),
        vm(3, LL, LL), vm(LL, L), vm(3, LL, LL), vm(3, LL, LL), vm(LL, LL),
        vm(c1, IMG, L, dtype=F32), vm(c2, IMG, L, dtype=F32), vm(c3, IMG, LL, dtype=F32),
        vm(c1, IMG, LL, dtype=F32), vm(c2, IMG, LL, dtype=F32), vm(c3, IMG, LL, dtype=F32),
        vm(c1 + 2, IMG, LL), vm(c2 + 2, IMG, LL), vm(c3 + 2, IMG, LL), vm(c2 + 1, 2, IMG, LL), vm(c3 + 1, 2, IMG, LL),
        vm(2, c3 * IMG, L, dtype=F32),
        *[packed] * 6,
        vm(c1 + 2, IMG, L), vm(c2 + 2, IMG, LL), vm(c3 + 2, IMG, LL), vm(c3 + 2, IMG, LL), vm(c2 + 1, 2, IMG, L), vm(c3 + 1, 2, IMG, L),
        pltpu.SemaphoreType.DMA((2,)), pltpu.SemaphoreType.DMA((9,)),
        pltpu.SemaphoreType.DMA((MESSAGES, N)), pltpu.SemaphoreType.DMA((MESSAGES, N)),
    ]

    def local(x_tile, *params):
        x_t = jnp.transpose(x_tile, (0, 1, 3, 2))
        params = [p.reshape(1, -1) if p.ndim == 1 else p for p in params]
        specs = [pl.BlockSpec(memory_space=pltpu.HBM)]
        for p in params:
            specs.append(pl.BlockSpec(memory_space=pltpu.VMEM if p.dtype == F32 else pltpu.HBM))
        return pl.pallas_call(
            functools.partial(_body, row_count),
            out_shape=jax.ShapeDtypeStruct((IMG, 1, 32, LL), BF),
            in_specs=specs,
            out_specs=pl.BlockSpec(memory_space=pltpu.VMEM),
            scratch_shapes=scratch,
            compiler_params=pltpu.CompilerParams(collective_id=0, has_side_effects=True, vmem_limit_bytes=60 * MIB),
        )(x_t, *params)

    return jax.shard_map(local, mesh=mesh, in_specs=(tile_spec,) + (P(),) * 15, out_specs=tile_spec, check_vma=False)
```

profile of v0, /device:TPU:1, one launch (start us, length us, event | category | flops | bytes accessed | tf_op | source)
XLA Modules:
  0.0 35.0 jit_solution(16418047938127725130)
XLA Ops:
  0.0 33.3 %shard_map.154 = bf16[16,1,32,256]{3,2,1,0:T(8,128)(2,1)} custom-call(bf16[16,8,32,256]{3,2,1,0:T(8,128)(2,1)} %bitcast.7, bf16[3,3,32,64]{3,2,1,0:T(8,128)(2,1)} %refs_1_.1, f32[1,64]{1,0:T(1,128)} %bitcast.10, bf16[3,3,64,64]{3,2,1,0:T(8,128)(2,1)} %refs_3_.1, f32[1,64]{1,0:T(1,128)} %bitcast.11, bf16[32,64]{1,0:T(8,128)(2,1)} %refs_5_.1, ...), custom_call_target="tpu_custom_call" | custom-call | tf_op jit(solution)/shard_map/pallas_call | solution.py:550
  33.3 1.7 %copy.18 = bf16[16,1,32,256]{3,2,1,0:T(8,128)(2,1)} copy(bf16[16,1,32,256]{3,2,1,0:T(8,128)(2,1)} %shard_map.154) | data formatting | bytes 524288
where the time goes:
time: 35.1 us; the launch traced here: 35 us
  Pallas kernels  33.3 us (95%)
  local copies, waits for them, and re-layouts  1.67 us (5%)
    pallas_call x1, Pallas kernels, local(): pl.pallas_call(functools.partial(_body, row_count), out_shape=jax.ShapeDt...  33.3 us
    unnamed x1, local copies, waits for them, and re-layouts  1.67 us

commit v1 on v0

--- a/solution.py
+++ b/solution.py
@@ -20,6 +20,7 @@
 IMG = 16
 N = 5
 PAD = 12
+NEED = (11, 7)
 COLS = (140, 70, 35)
 M = tuple(p // N for p in COLS)
 MH = M[0] // 2
@@ -27,7 +28,7 @@
 TAPS = range(3)
 MIB = 1024 * 1024
 
-(X_TOP, X_COL, Y1_DOWN, Y1_UP, Z1_DOWN, Y2_DOWN, Y2_UP, Z2_DOWN, Y3_DOWN, Y3_UP, MESSAGES) = range(11)
+(X_TOP, X_COL, Y1_DOWN, Y1_UP, Z1_DOWN, Y2_DOWN, Z1_UP, Z2_DOWN, Y3_DOWN, Y3_UP, MESSAGES) = range(11)
 
 
 def _dot(a, b):
@@ -51,14 +52,14 @@
 
 
 def _body(row_count, *refs):
-    (x_hbm, wd1_h, bd1, wc1_h, bc1, wp1_h, wd2_h, bd2, wc2_h, bc2, wp2_h, wd3_h, bd3, wc3_h, bc3, wp3_h,
+    (x_hbm, wd1_h, bd1_h, wc1_h, bc1_h, wp1_h, wd2_h, bd2_h, wc2_h, bc2_h, wp2_h, wd3_h, bd3_h, wc3_h, bc3_h, wp3_h,
      out_ref,
      xv, xt, xtop, xh, fs, sdiag, rdiag, bias,
-     wd1r, wc1r, wp1r, wd2r, wc2r, wp2r, wd3, wc3, wp3,
-     wd1, wdh1, wc1, wch1, wpp1, wd2, wdh2, wc2, wch2, wpp2,
+     wd1r, wc1r, wp1r, wd2r, wc2r, wp2r, wd3, wc3, wp3, bd1, bc1, bd2, bc2, bd3, bc3,
+     wd1, wdh1, wc1, wch1, wpp1, wd2, wdh2, wdb2, wc2, wch2, wpp2,
      part1, part2, part3, acc1, acc2, acc3, y1, y2, y3, z1, z2, zo,
      sy1d, sy1u, sz1, ry1d, ry1u, rz1,
-     yh1, yh2, yt3, yb3, zh1, zh2,
+     yh1, yh2, yt3, yb3, zh1, zb1, zh2,
      xsem, wsem, ssem, rsem) = refs
 
     row = lax.axis_index("row")
@@ -93,20 +94,21 @@
         return pltpu.make_async_copy(x_hbm.at[:, :, :, pl.ds(pl.multiple_of(h * L, L), L)], xv.at[h], xsem.at[h])
 
     w_copies = [pltpu.make_async_copy(s, d, wsem.at[i]) for i, (s, d) in enumerate(
-        ((wd1_h, wd1r), (wc1_h, wc1r), (wp1_h, wp1r), (wd2_h, wd2r), (wc2_h, wc2r), (wp2_h, wp2r),
+        ((wd1_h, wd1r), (bd1_h, bd1), (bc1_h, bc1), (bd2_h, bd2), (bc2_h, bc2), (bd3_h, bd3), (bc3_h, bc3),
+         (wc1_h, wc1r), (wp1_h, wp1r), (wd2_h, wd2r), (wc2_h, wc2r), (wp2_h, wp2r),
          (wd3_h, wd3), (wc3_h, wc3), (wp3_h, wp3)))]
-    w_copies[0].start()
+    first_copies, late_copies = w_copies[:7], w_copies[7:]
     x_copy(inner).start()
+    for c in first_copies:
+        c.start()
     x_copy(outer).start()
-    for c in w_copies[1:]:
-        c.start()
 
     def remote(src, dst, msg, k, dev):
         return pltpu.make_async_remote_copy(src_ref=src, dst_ref=dst, send_sem=ssem.at[msg, k], recv_sem=rsem.at[msg, k],
                                             device_id=dev, device_id_type=MESH)
 
     def m_xtop(h):
-        return remote(x_hbm.at[:, 7, :, pl.ds(pl.multiple_of(h * L, L), L)], xtop.at[h], X_TOP, h, down)
+        return remote(xv.at[h, :, 7], xtop.at[h], X_TOP, h, down)
 
     def m_diag():
         return remote(sdiag, rdiag, X_TOP, 2, diag_down)
@@ -114,8 +116,15 @@
     own_edge = 1 + (L - PAD) * inner + PAD * col
     far_edge = 1 + L * col
 
-    def m_xcol():
-        return remote(xt.at[pl.ds(own_edge, PAD)], xt.at[pl.ds(far_edge, PAD)], X_COL, 0, side)
+    def m_xcol(c):
+        skip = (PAD - NEED[0]) * (1 - c)
+        return remote(xt.at[pl.ds(own_edge + skip, NEED[c])], xt.at[pl.ds(far_edge + skip, NEED[c])], X_COL, 0, side)
+
+    def for_col(fn):
+        for c in range(2):
+            @pl.when(col == c)
+            def _():
+                fn(c)
 
     def plain(src, dst, msg, dev, first, size, src_lanes=None, dst_lanes=None):
         def make(k):
@@ -132,9 +141,12 @@
     m_y1u = plain(sy1u, ry1u, Y1_UP, up, 0, MH)
     m_z1 = plain(sz1, rz1, Z1_DOWN, down, 0, MH)
     m_y2d = plain(y2, yh2, Y2_DOWN, down, 1, M[1], lanes_hi, lanes_lo)
-    m_y2u = plain(y2, yh2, Y2_UP, up, 1, M[1], lanes_lo, lanes_hi)
     m_y3d = plain(y3, yt3, Y3_DOWN, down, 1, M[2])
     m_y3u = plain(y3, yb3, Y3_UP, up, 1, M[2])
+
+    def m_z1u(k):
+        s = pl.ds(1 + order(k) * MH, MH)
+        return remote(z1.at[s, :, :, lanes_lo], zb1.at[s], Z1_UP, k, up)
 
     def m_z2(k):
         s = pl.ds(1 + order(k) * M[2], M[2])
@@ -164,19 +176,20 @@
                 for m in ups:
                     m(k).wait_recv()
 
-    for ref in (xt, xh, z1, z2, zh1, zh2, y1, y2, y3, yh1, yh2, yt3, yb3):
+    for ref in (xt, xh, z1, z2, zh1, zb1, zh2, y1, y2, y3, yh1, yh2, yt3, yb3):
         ref[0] = jnp.zeros(ref.shape[1:], BF)
     for ref in (y1, y2, y3, yh1, yh2, yt3, yb3):
         ref[ref.shape[0] - 1] = jnp.zeros(ref.shape[1:], BF)
-    for i, (b, reps) in enumerate(((bd1, 4), (bc1, 4), (bd2, 2), (bc2, 2), (bd3, 1), (bc3, 1))):
-        v = jnp.concatenate([b[...]] * reps, axis=-1)
-        bias[i] = jnp.broadcast_to(v, (IMG, LL))
 
     neighbours = 1 + 2 * jnp.minimum(row, 1) + 2 * jnp.minimum(row_count - 1 - row, 1)
     pl.semaphore_wait(barrier, neighbours)
 
+    x_copy(outer).wait()
+    x_copy(inner).wait()
     send([m_xtop], [], outer)
     send([m_xtop], [], inner)
+    for c in late_copies:
+        c.start()
 
     @pl.when(jnp.logical_not(has_up))
     def _():
@@ -186,9 +199,8 @@
 
     @pl.when(jnp.logical_not(has_down))
     def _():
-        for ref in (ry1u, yb3):
+        for ref in (ry1u, zb1, yb3):
             ref[...] = jnp.zeros(ref.shape, BF)
-        yh2[:, :, HI] = jnp.zeros((yh2.shape[0], IMG, L), BF)
 
     def toeplitz(dst, rows_in, rows_out, shape, piece):
         for r in range(rows_in):
@@ -204,7 +216,11 @@
             return w[kh, kw] if kh in TAPS else None
         return piece
 
-    w_copies[0].wait()
+    for c in first_copies:
+        c.wait()
+    for i, (b, reps) in enumerate(((bd1, 4), (bc1, 4), (bd2, 2), (bc2, 2), (bd3, 1), (bc3, 1))):
+        v = jnp.concatenate([b[...]] * reps, axis=-1)
+        bias[i] = jnp.broadcast_to(v, (IMG, LL))
     s_d1, s_c1 = wd1r.shape[2:], wc1r.shape[2:]
     for kw in TAPS:
         toeplitz(wd1.at[kw], 8, 4, s_d1, tap_of(wd1r, kw, 2))
@@ -215,10 +231,13 @@
             for g in range(2):
                 block = xv[h, n, 4 * g:4 * g + 4].reshape(L, L)
                 fs[g, n * STEP:n * STEP + L, :] = block.T.astype(F32)
+
+    def gather_pairs(h, lo, n):
         base = 1 + PAD * col + H * h
 
-        @pl.loop(0, H, unroll=8)
-        def _(p):
+        @pl.loop(0, n, unroll=4)
+        def _(i):
+            p = lo + i
             for e in range(2):
                 v = [fs[g, pl.ds(2 * p + e, IMG, stride=STEP), :] for g in range(2)]
                 xt[base + p, e] = jnp.concatenate(v, axis=-1).astype(BF)
@@ -255,17 +274,19 @@
         u = jnp.stack(out, axis=1).astype(BF)
         xh[pl.ds(1 + L * (1 - col), PAD)] = u.reshape(PAD, 2, IMG, L)
 
-    x_copy(inner).wait()
+    border = (H - PAD) * inner
     transpose_half(inner)
-    m_xcol().start()
+    gather_pairs(inner, border, PAD)
+    for_col(lambda c: m_xcol(c).start())
     pack_diag()
 
     @pl.when(has_down)
     def _():
         m_diag().start()
 
-    x_copy(outer).wait()
+    gather_pairs(inner, PAD * col, H - PAD)
     transpose_half(outer)
+    gather_pairs(outer, 0, H)
 
     def taps(ref, j0, m):
         return [_flat(ref[pl.ds(j0 + t, m)]) for t in TAPS]
@@ -346,6 +367,13 @@
         v = tiles(_dot(t, wdh2[...]), m2) + part2[pl.ds(j0, m2)]
         y2[pl.ds(1 + j0, m2), :, LO] = _relu(v + bias[2, :, LO]).astype(BF)
 
+    def bottom2(k):
+        j0 = order(k) * m2
+        own, below = pair_taps(z1, j0, m2), pair_taps(zb1, j0, m2)
+        lhs = [jnp.concatenate([a[:, HI], b], axis=-1) for a, b in zip(own, below)]
+        v = _relu(tiles(sum_dots(lhs, lambda t: wdb2[t]), m2) + bias[2, :, LO])
+        yh2[pl.ds(1 + j0, m2), :, HI] = jnp.where(has_down, v, 0.0).astype(BF)
+
     def conv2(k):
         j0 = order(k) * m2
         v = sum_dots(taps(y2, j0, m2), lambda t: wc2[t]) + _dot(_flat(z1[pl.ds(j0 + 1, m2), 0]), wpp2[...])
@@ -354,6 +382,12 @@
     def halo2(k):
         j0 = order(k) * m2
         v = tiles(sum_dots(taps(yh2, j0, m2), lambda t: wch2[t]), m2) + acc2[pl.ds(j0, m2)]
+        z2[pl.ds(1 + order(k) * m3, m3)] = _relu(v).astype(BF).reshape(m3, 2, IMG, LL)
+
+    def full2(k):
+        j0 = order(k) * m2
+        v = sum_dots(taps(y2, j0, m2), lambda t: wc2[t]) + _dot(_flat(z1[pl.ds(j0 + 1, m2), 0]), wpp2[...])
+        v = tiles(v + sum_dots(taps(yh2, j0, m2), lambda t: wch2[t]), m2) + bias[3]
         z2[pl.ds(1 + order(k) * m3, m3)] = _relu(v).astype(BF).reshape(m3, 2, IMG, LL)
 
     def down3(k):
@@ -387,112 +421,120 @@
         if k < last:
             recv(downs, ups, k + 1)
 
-    for k in range(N - 1):
+    for k in range(last):
         down1(k)
+    for k in range(last):
         send([m_y1d], [], k)
 
-    recv([m_xtop], [], outer)
-    transpose_top(outer)
-    for k in range(2):
-        top1(k)
-        send([], [m_y1u], k)
-
-    for c in w_copies[1:]:
+    for c in late_copies:
         c.wait()
     for kw in TAPS:
         toeplitz(wc1.at[kw], 4, 4, s_c1, tap_of(wc1r, kw, 1))
+        toeplitz(wch1.at[kw], 2, 4, s_c1, lambda r, i: wc1r[2 * r, kw] if i == 3 * r else None)
     toeplitz(wpp1, 8, 4, s_d1, lambda r, i: wp1r[...] if r == 2 * i else None)
-
-    recv([m_xtop], [], inner)
-    transpose_top(inner)
-    for k in range(2, N - 1):
-        conv1(k - 2)
-        top1(k)
-        send([], [m_y1u], k)
-
-    for kw in TAPS:
-        toeplitz(wch1.at[kw], 2, 4, s_c1, lambda r, i: wc1r[2 * r, kw] if i == 3 * r else None)
-    m_xcol().wait_recv()
-    conv1(2)
-    down1(last)
-    send([m_y1d], [], last)
-
-    @pl.when(has_up)
-    def _():
-        m_diag().wait_recv()
-
-    unpack_diag()
-    top1(last)
-    send([], [m_y1u], last)
 
     s_d2, s_c2 = wd2r.shape[2:], wc2r.shape[2:]
     for kw in TAPS:
         toeplitz(wd2.at[kw], 4, 2, s_d2, tap_of(wd2r, kw, 2))
+        toeplitz(wdb2.at[kw], 4, 1, s_d2, lambda r, i: wd2r[r - 1, kw] if r else None)
         toeplitz(wc2.at[kw], 2, 2, s_c2, tap_of(wc2r, kw, 1))
         toeplitz(wch2.at[kw], 2, 2, s_c2, lambda r, i: wc2r[2 * r, kw] if i == r else None)
     toeplitz(wpp2, 4, 2, s_d2, lambda r, i: wp2r[...] if r == 2 * i else None)
     toeplitz(wdh2, 4, 1, s_d2, lambda r, i: wd2r[0, r] if r in TAPS else None)
 
-    conv1(3)
+    recv([m_xtop], [], outer)
+    transpose_top(outer)
+    top1(0)
+    send([], [m_y1u], 0)
+    top1(1)
+    send([], [m_y1u], 1)
+
+    recv([m_xtop], [], inner)
+    transpose_top(inner)
+    top1(2)
+    top1(3)
+    send([], [m_y1u], 2)
+    send([], [m_y1u], 3)
+    conv1(0)
+
+    @pl.when(has_up)
+    def _():
+        m_diag().wait_recv()
+
+    unpack_diag()
+    for_col(lambda c: m_xcol(1 - c).wait_recv())
+    down1(last)
+    top1(last)
+    send([m_y1d], [m_y1u], last)
+
     recv([m_y1d], [m_y1u], 0)
     unpack1(0)
     for k in range(N):
         if k < last:
             recv([m_y1d], [m_y1u], k + 1)
             unpack1(k + 1)
-        if k == 0:
-            conv1(last)
         if k >= 2:
             down2(k - 2)
         halo1(k)
-        send([m_z1], [], k)
+        if k < last:
+            conv1(k + 1)
+        send([m_z1], [m_z1u], k)
         if k >= 2:
             send([m_y2d], [], k - 2)
-
-    recv([m_z1], [], 0)
+    down2(3)
+    down2(last)
+    send([m_y2d], [], 3)
+    send([m_y2d], [], last)
+
+    recv([m_z1], [m_z1u], 0)
     unpack2(0)
+    for k in range(3):
+        recv([m_z1], [m_z1u], k + 1)
+        unpack2(k + 1)
+        top2(k)
+        bottom2(k)
+        if k:
+            wait_next([m_y2d], [], k - 1)
+            full2(k - 1)
+            send([m_z2], [], k - 1)
+    recv([m_z1], [m_z1u], last)
+    unpack2(last)
+    top2(3)
+    bottom2(3)
+    top2(last)
+    bottom2(last)
+    recv([m_y2d], [], 3)
+    full2(2)
+    send([m_z2], [], 2)
+    recv([m_y2d], [], last)
+    full2(3)
+    full2(last)
+    send([m_z2], [], 3)
+    send([m_z2], [], last)
+
     for k in range(N):
-        if k < last:
-            recv([m_z1], [], k + 1)
-            unpack2(k + 1)
-        if k < 2:
-            down2(k + 3)
-        else:
-            conv2(k - 2)
-        top2(k)
-        send([], [m_y2u], k)
-        if k < 2:
-            send([m_y2d], [], k + 3)
-
-    for k in range(N):
-        wait_next([m_y2d], [m_y2u], k)
-        if k < 2:
-            conv2(k + 3)
-        else:
-            down3(k - 2)
-        halo2(k)
-        send([m_z2], [], k)
-
+        down3(k)
     for k in range(N):
         wait_next([m_z2], [], k)
-        if k < 2:
-            down3(k + 3)
-        else:
+        if k >= 2:
             conv3(k - 2)
         top3(k)
         send([m_y3d], [m_y3u], k)
-
-    for k in range(N):
+    conv3(3)
+    conv3(last)
+    for k in range(3):
         wait_next([m_y3d], [m_y3u], k)
-        if k < 2:
-            conv3(k + 3)
+    for k in range(3):
         halo3(k)
+    wait_next([m_y3d], [m_y3u], 3)
+    halo3(3)
+    halo3(last)
 
     for n in range(IMG):
         v = [zo[g, pl.ds(PAD * 4 * col + n, out_ref.shape[2], stride=IMG), :] for g in range(2)]
         out_ref[n, 0] = jnp.concatenate(v, axis=-1).astype(BF)
 
-    m_xcol().wait_send()
+    for_col(lambda c: m_xcol(c).wait_send())
 
     @pl.when(has_down)
     def _():
@@ -509,7 +551,7 @@
     def _():
         @pl.loop(0, N)
         def _(k):
-            for m in (m_y1u, m_y2u, m_y3u):
+            for m in (m_y1u, m_z1u, m_y3u):
                 m(k).wait_send()
 
 
@@ -529,31 +571,30 @@
         vm(2, IMG, 8, Q, L), vm(c1 + 1, 2, IMG, LL), vm(2, IMG, Q, L), vm(c1 + 1, 2, IMG, L),
         vm(2, IMG * STEP, L, dtype=F32), vm(PAD // 2, IMG, L), vm(PAD // 2, IMG, L), vm(6, IMG, LL, dtype=F32),
         *weights(Q, H), *weights(H, L), *weights(L, LL),
+        *[vm(1, c, dtype=F32) for c in (H, H, L, L, LL, LL)],
         vm(3, LL, LL), vm(L, L), vm(3, LL, LL), vm(3, L, LL), vm(LL, LL),
-        vm(3, LL, LL), vm(LL, L), vm(3, LL, LL), vm(3, LL, LL), vm(LL, LL),
+        vm(3, LL, LL), vm(LL, L), vm(3, LL, L), vm(3, LL, LL), vm(3, LL, LL), vm(LL, LL),
         vm(c1, IMG, L, dtype=F32), vm(c2, IMG, L, dtype=F32), vm(c3, IMG, LL, dtype=F32),
         vm(c1, IMG, LL, dtype=F32), vm(c2, IMG, LL, dtype=F32), vm(c3, IMG, LL, dtype=F32),
         vm(c1 + 2, IMG, LL), vm(c2 + 2, IMG, LL), vm(c3 + 2, IMG, LL), vm(c2 + 1, 2, IMG, LL), vm(c3 + 1, 2, IMG, LL),
         vm(2, c3 * IMG, L, dtype=F32),
         *[packed] * 6,
-        vm(c1 + 2, IMG, L), vm(c2 + 2, IMG, LL), vm(c3 + 2, IMG, LL), vm(c3 + 2, IMG, LL), vm(c2 + 1, 2, IMG, L), vm(c3 + 1, 2, IMG, L),
-        pltpu.SemaphoreType.DMA((2,)), pltpu.SemaphoreType.DMA((9,)),
+        vm(c1 + 2, IMG, L), vm(c2 + 2, IMG, LL), vm(c3 + 2, IMG, LL), vm(c3 + 2, IMG, LL), vm(c2 + 1, 2, IMG, L), vm(c2 + 1, 2, IMG, L), vm(c3 + 1, 2, IMG, L),
+        pltpu.SemaphoreType.DMA((2,)), pltpu.SemaphoreType.DMA((15,)),
         pltpu.SemaphoreType.DMA((MESSAGES, N)), pltpu.SemaphoreType.DMA((MESSAGES, N)),
     ]
 
     def local(x_tile, *params):
         x_t = jnp.transpose(x_tile, (0, 1, 3, 2))
         params = [p.reshape(1, -1) if p.ndim == 1 else p for p in params]
-        specs = [pl.BlockSpec(memory_space=pltpu.HBM)]
-        for p in params:
-            specs.append(pl.BlockSpec(memory_space=pltpu.VMEM if p.dtype == F32 else pltpu.HBM))
+        operands = [pltpu.with_memory_space_constraint(p, pltpu.HBM) for p in (x_t, *params)]
         return pl.pallas_call(
             functools.partial(_body, row_count),
-            out_shape=jax.ShapeDtypeStruct((IMG, 1, 32, LL), BF),
-            in_specs=specs,
+            out_shape=pltpu.VMEM((IMG, 1, 32, LL), BF),
+            in_specs=[pl.BlockSpec(memory_space=pltpu.HBM)] * len(operands),
             out_specs=pl.BlockSpec(memory_space=pltpu.VMEM),
             scratch_shapes=scratch,
             compiler_params=pltpu.CompilerParams(collective_id=0, has_side_effects=True, vmem_limit_bytes=60 * MIB),
-        )(x_t, *params)
+        )(*operands)
 
     return jax.shard_map(local, mesh=mesh, in_specs=(tile_spec,) + (P(),) * 15, out_specs=tile_spec, check_vma=False)

time: 35.1 us -> 30.5 us (0.87)
  Pallas kernels: 33.3 us -> 29.7 us
  local copies, waits for them, and re-layouts: 1.67 us -> 0.71 us
    pallas_call x1, Pallas kernels: 33.3 us -> 29.7 us  [local(): pl.pallas_call(functools.partial(_body, row_count), out_shape=pltpu.VMEM(...]
    unnamed x1, local copies, waits for them, and re-layouts: 1.67 us -> 0.71 us
where the time goes in v1:
time: 30.5 us; the launch traced here: 30.4 us
  Pallas kernels  29.7 us (97%)
  local copies, waits for them, and re-layouts  0.71 us (2%)
    pallas_call x1, Pallas kernels, local(): pl.pallas_call(functools.partial(_body, row_count), out_shape=pltpu.VMEM(...  29.7 us
    unnamed x1, local copies, waits for them, and re-layouts  0.71 us

profile of v1, /device:TPU:1, one launch (start us, length us, event | category | flops | bytes accessed | tf_op | source)
XLA Modules:
  0.0 30.4 jit_solution(14700982534396814359)
XLA Ops:
  0.0 29.7 %shard_map.154 = bf16[16,1,32,256]{3,2,1,0:T(8,128)(2,1)S(1)} custom-call(bf16[16,8,32,256]{3,2,1,0:T(8,128)(2,1)} %bitcast.7, bf16[3,3,32,64]{3,2,1,0:T(8,128)(2,1)} %refs_1_.1, f32[1,64]{1,0:T(1,128)} %bitcast.10, bf16[3,3,64,64]{3,2,1,0:T(8,128)(2,1)} %refs_3_.1, f32[1,64]{1,0:T(1,128)} %bitcast.11, bf16[32,64]{1,0:T(8,128)(2,1)} %refs_5_.1, ...), custom_call_target="tpu_custom_call" | custom-call | tf_op jit(solution)/shard_map/pallas_call | solution.py:591
  29.7 0.7 %copy.18 = bf16[16,1,32,256]{3,2,1,0:T(8,128)(2,1)} copy(bf16[16,1,32,256]{3,2,1,0:T(8,128)(2,1)S(1)} %shard_map.154) | data formatting | bytes 524288

commit v2 on v1

--- a/solution.py
+++ b/solution.py
@@ -60,7 +60,7 @@
      part1, part2, part3, acc1, acc2, acc3, y1, y2, y3, z1, z2, zo,
      sy1d, sy1u, sz1, ry1d, ry1u, rz1,
      yh1, yh2, yt3, yb3, zh1, zb1, zh2,
-     xsem, wsem, ssem, rsem) = refs
+     xsem, wsem, ssem, rsem, near_sem) = refs
 
     row = lax.axis_index("row")
     col = lax.axis_index("col")
@@ -71,7 +71,6 @@
     down = {"row": row + 1}
     side = {"col": 1 - col}
     diag_down = {"row": row + 1, "col": 1 - col}
-    diag_up = {"row": row - 1, "col": 1 - col}
 
     barrier = pltpu.get_barrier_semaphore()
 
@@ -83,12 +82,10 @@
     @pl.when(has_up)
     def _():
         greet(up)
-        greet(diag_up)
 
     @pl.when(has_down)
     def _():
         greet(down)
-        greet(diag_down)
 
     def x_copy(h):
         return pltpu.make_async_copy(x_hbm.at[:, :, :, pl.ds(pl.multiple_of(h * L, L), L)], xv.at[h], xsem.at[h])
@@ -126,9 +123,14 @@
             def _():
                 fn(c)
 
-    def plain(src, dst, msg, dev, first, size, src_lanes=None, dst_lanes=None):
+    def chunk(k, size, need):
+        if k == N - 1:
+            return pl.ds(1 + order(k) * size + (size - need) * col, need)
+        return pl.ds(1 + order(k) * size, size)
+
+    def plain(src, dst, msg, dev, size, need, src_lanes=None, dst_lanes=None):
         def make(k):
-            s = pl.ds(first + order(k) * size, size)
+            s = chunk(k, size, need)
             return remote(src.at[s] if src_lanes is None else src.at[s, :, src_lanes],
                           dst.at[s] if dst_lanes is None else dst.at[s, :, dst_lanes], msg, k, dev)
         return make
@@ -137,19 +139,25 @@
         return k + col * (N - 1 - 2 * k)
 
     lanes_lo, lanes_hi = pl.ds(0, L), pl.ds(L, L)
-    m_y1d = plain(sy1d, ry1d, Y1_DOWN, down, 0, MH)
-    m_y1u = plain(sy1u, ry1u, Y1_UP, up, 0, MH)
-    m_z1 = plain(sz1, rz1, Z1_DOWN, down, 0, MH)
-    m_y2d = plain(y2, yh2, Y2_DOWN, down, 1, M[1], lanes_hi, lanes_lo)
-    m_y3d = plain(y3, yt3, Y3_DOWN, down, 1, M[2])
-    m_y3u = plain(y3, yb3, Y3_UP, up, 1, M[2])
+    def packed(src, dst, msg, dev):
+        def make(k):
+            s = pl.ds(order(k) * MH, MH)
+            return remote(src.at[s], dst.at[s], msg, k, dev)
+        return make
+
+    m_y1d = packed(sy1d, ry1d, Y1_DOWN, down)
+    m_y1u = packed(sy1u, ry1u, Y1_UP, up)
+    m_z1 = packed(sz1, rz1, Z1_DOWN, down)
+    m_y2d = plain(y2, yh2, Y2_DOWN, down, M[1], 12, lanes_hi, lanes_lo)
+    m_y3d = plain(y3, yt3, Y3_DOWN, down, M[2], 5)
+    m_y3u = plain(y3, yb3, Y3_UP, up, M[2], 5)
 
     def m_z1u(k):
-        s = pl.ds(1 + order(k) * MH, MH)
+        s = chunk(k, MH, 13)
         return remote(z1.at[s, :, :, lanes_lo], zb1.at[s], Z1_UP, k, up)
 
     def m_z2(k):
-        s = pl.ds(1 + order(k) * M[2], M[2])
+        s = chunk(k, M[2], 6)
         return remote(z2.at[s, :, :, lanes_hi], zh2.at[s], Z2_DOWN, k, down)
 
     def send(downs, ups, k):
@@ -181,13 +189,21 @@
     for ref in (y1, y2, y3, yh1, yh2, yt3, yb3):
         ref[ref.shape[0] - 1] = jnp.zeros(ref.shape[1:], BF)
 
-    neighbours = 1 + 2 * jnp.minimum(row, 1) + 2 * jnp.minimum(row_count - 1 - row, 1)
-    pl.semaphore_wait(barrier, neighbours)
+    vertical = jnp.minimum(row, 1) + jnp.minimum(row_count - 1 - row, 1)
+    pl.semaphore_wait(barrier, 1 + vertical)
 
     x_copy(outer).wait()
     x_copy(inner).wait()
     send([m_xtop], [], outer)
     send([m_xtop], [], inner)
+    @pl.when(has_up)
+    def _():
+        pl.semaphore_signal(near_sem, inc=1, device_id=up, device_id_type=MESH)
+
+    @pl.when(has_down)
+    def _():
+        pl.semaphore_signal(near_sem, inc=1, device_id=down, device_id_type=MESH)
+
     for c in late_copies:
         c.start()
 
@@ -279,14 +295,14 @@
     gather_pairs(inner, border, PAD)
     for_col(lambda c: m_xcol(c).start())
     pack_diag()
-
-    @pl.when(has_down)
-    def _():
-        m_diag().start()
-
     gather_pairs(inner, PAD * col, H - PAD)
     transpose_half(outer)
     gather_pairs(outer, 0, H)
+    pl.semaphore_wait(near_sem, vertical)
+
+    @pl.when(has_down)
+    def _():
+        m_diag().start()
 
     def taps(ref, j0, m):
         return [_flat(ref[pl.ds(j0 + t, m)]) for t in TAPS]
@@ -300,6 +316,10 @@
             v = v + _dot(lhs[t], w(t))
         return v
 
+    def sum_narrow(lhs, w):
+        pair = jnp.concatenate([w(0), w(1)], axis=0)
+        return _dot(jnp.concatenate(lhs[:2], axis=-1), pair) + _dot(lhs[2], w(2))
+
     def tiles(v, m):
         return v.reshape(m, IMG, v.shape[-1])
 
@@ -310,22 +330,30 @@
 
     m1, m2, m3 = M
 
-    def down1(k):
+    def above1(j0):
+        a, b, c = pair_taps(xh, j0, m1)
+        ln = _lane(a.shape)
+        return tiles(_dot(jnp.where(ln < Q, a, jnp.where(ln < H, b, c)), wdh1[...]), m1)
+
+    def store_top1(k, v):
+        lo = _relu(v + bias[0, :, LO])
+        y1[pl.ds(1 + order(k) * m1, m1), :, LO] = lo.astype(BF)
+        sy1u[pl.ds(order(k) * MH, MH)] = pack(lo[:MH], _roll(lo[MH:], H))
+
+    def down1(k, whole=False):
         j0 = order(k) * m1
         v = tiles(sum_dots(pair_taps(xt, j0, m1), lambda t: wd1[t]), m1)
-        part1[pl.ds(j0, m1)] = v[:, :, LO]
+        if whole:
+            store_top1(k, v[:, :, LO] + above1(j0))
+        else:
+            part1[pl.ds(j0, m1)] = v[:, :, LO]
         hi = _relu(v[:, :, HI] + bias[0, :, HI])
         y1[pl.ds(1 + j0, m1), :, HI] = hi.astype(BF)
         sy1d[pl.ds(order(k) * MH, MH)] = pack(_roll(hi[:MH], H), hi[MH:])
 
     def top1(k):
         j0 = order(k) * m1
-        a, b, c = pair_taps(xh, j0, m1)
-        ln = _lane(a.shape)
-        v = tiles(_dot(jnp.where(ln < Q, a, jnp.where(ln < H, b, c)), wdh1[...]), m1)
-        lo = _relu(v + part1[pl.ds(j0, m1)] + bias[0, :, LO])
-        y1[pl.ds(1 + j0, m1), :, LO] = lo.astype(BF)
-        sy1u[pl.ds(order(k) * MH, MH)] = pack(lo[:MH], _roll(lo[MH:], H))
+        store_top1(k, above1(j0) + part1[pl.ds(j0, m1)])
 
     def conv1(k):
         j0 = order(k) * m1
@@ -340,7 +368,7 @@
 
     def halo1(k):
         j0 = order(k) * m1
-        v = tiles(sum_dots(taps(yh1, j0, m1), lambda t: wch1[t]), m1)
+        v = tiles(sum_narrow(taps(yh1, j0, m1), lambda t: wch1[t]), m1)
         v = _relu(v + acc1[pl.ds(j0, m1)])
         z1[pl.ds(1 + order(k) * MH, MH)] = v.astype(BF).reshape(MH, 2, IMG, LL)
         hi = v[:, :, HI]
@@ -384,12 +412,6 @@
         v = tiles(sum_dots(taps(yh2, j0, m2), lambda t: wch2[t]), m2) + acc2[pl.ds(j0, m2)]
         z2[pl.ds(1 + order(k) * m3, m3)] = _relu(v).astype(BF).reshape(m3, 2, IMG, LL)
 
-    def full2(k):
-        j0 = order(k) * m2
-        v = sum_dots(taps(y2, j0, m2), lambda t: wc2[t]) + _dot(_flat(z1[pl.ds(j0 + 1, m2), 0]), wpp2[...])
-        v = tiles(v + sum_dots(taps(yh2, j0, m2), lambda t: wch2[t]), m2) + bias[3]
-        z2[pl.ds(1 + order(k) * m3, m3)] = _relu(v).astype(BF).reshape(m3, 2, IMG, LL)
-
     def down3(k):
         j0 = order(k) * m3
         v = sum_dots(pair_taps(z2, j0, m3), lambda t: wd3[1:, t].reshape(LL, LL))
@@ -397,7 +419,7 @@
 
     def top3(k):
         j0 = order(k) * m3
-        v = tiles(sum_dots(pair_taps(zh2, j0, m3), lambda t: wd3[0, t]), m3) + part3[pl.ds(j0, m3)]
+        v = tiles(sum_narrow(pair_taps(zh2, j0, m3), lambda t: wd3[0, t]), m3) + part3[pl.ds(j0, m3)]
         y3[pl.ds(1 + j0, m3)] = _relu(v).astype(BF)
 
     def conv3(k):
@@ -457,19 +479,28 @@
     send([], [m_y1u], 3)
     conv1(0)
 
-    @pl.when(has_up)
-    def _():
-        m_diag().wait_recv()
-
-    unpack_diag()
-    for_col(lambda c: m_xcol(1 - c).wait_recv())
-    down1(last)
-    top1(last)
-    send([m_y1d], [m_y1u], last)
-
-    recv([m_y1d], [m_y1u], 0)
-    unpack1(0)
-    for k in range(N):
+    def border1():
+        @pl.when(has_up)
+        def _():
+            m_diag().wait_recv()
+
+        for_col(lambda c: m_xcol(1 - c).wait_recv())
+        unpack_diag()
+        down1(last, True)
+        send([m_y1d], [m_y1u], last)
+
+    def first_z1():
+        for k in range(2):
+            recv([m_y1d], [m_y1u], k)
+            unpack1(k)
+        halo1(0)
+        conv1(1)
+        send([m_z1], [m_z1u], 0)
+
+    border1()
+    first_z1()
+
+    for k in range(1, N):
         if k < last:
             recv([m_y1d], [m_y1u], k + 1)
             unpack1(k + 1)
@@ -479,60 +510,81 @@
         if k < last:
             conv1(k + 1)
         send([m_z1], [m_z1u], k)
-        if k >= 2:
-            send([m_y2d], [], k - 2)
+    for k in range(3):
+        send([m_y2d], [], k)
     down2(3)
     down2(last)
     send([m_y2d], [], 3)
     send([m_y2d], [], last)
 
-    recv([m_z1], [m_z1u], 0)
-    unpack2(0)
-    for k in range(3):
-        recv([m_z1], [m_z1u], k + 1)
-        unpack2(k + 1)
+    def above2(k):
+        if k == 0:
+            recv([m_z1], [], 0)
+            unpack2(0)
+        if k < last:
+            recv([m_z1], [], k + 1)
+            unpack2(k + 1)
+        if k >= 2:
+            conv2(k - 2)
         top2(k)
+
+    above2(0)
+    above2(1)
+    recv([], [m_z1u], 0)
+    for k in range(last):
+        if k + 2 < N:
+            above2(k + 2)
+        else:
+            conv2(3)
+            conv2(last)
+        recv([], [m_z1u], k + 1)
         bottom2(k)
+        if k == last - 1:
+            bottom2(last)
         if k:
             wait_next([m_y2d], [], k - 1)
-            full2(k - 1)
+            if k == last - 1:
+                down3(0)
+            halo2(k - 1)
             send([m_z2], [], k - 1)
-    recv([m_z1], [m_z1u], last)
-    unpack2(last)
-    top2(3)
-    bottom2(3)
-    top2(last)
-    bottom2(last)
-    recv([m_y2d], [], 3)
-    full2(2)
-    send([m_z2], [], 2)
     recv([m_y2d], [], last)
-    full2(3)
-    full2(last)
+    down3(1)
+    halo2(3)
+    halo2(last)
     send([m_z2], [], 3)
     send([m_z2], [], last)
 
+    recv([m_z2], [], 0)
+    for k in range(3):
+        recv([m_z2], [], k + 1)
+        top3(k)
+        down3(k + 2)
+        send([m_y3d], [m_y3u], k)
+    recv([m_z2], [], last)
+    top3(3)
+    top3(last)
+    send([m_y3d], [m_y3u], 3)
+    send([m_y3d], [m_y3u], last)
     for k in range(N):
-        down3(k)
-    for k in range(N):
-        wait_next([m_z2], [], k)
-        if k >= 2:
-            conv3(k - 2)
-        top3(k)
-        send([m_y3d], [m_y3u], k)
-    conv3(3)
-    conv3(last)
+        conv3(k)
+
+    half = IMG
+
+    def write_out(h):
+        lo = pl.multiple_of(half * h, half)
+        for n in range(IMG):
+            v = [zo[g, pl.ds(PAD * 4 * col + half * IMG * h + n, half, stride=IMG), :] for g in range(2)]
+            out_ref[n, 0, pl.ds(lo, half)] = jnp.concatenate(v, axis=-1).astype(BF)
+
     for k in range(3):
         wait_next([m_y3d], [m_y3u], k)
     for k in range(3):
         halo3(k)
-    wait_next([m_y3d], [m_y3u], 3)
+    write_out(outer)
+    recv([m_y3d], [m_y3u], last)
     halo3(3)
     halo3(last)
-
-    for n in range(IMG):
-        v = [zo[g, pl.ds(PAD * 4 * col + n, out_ref.shape[2], stride=IMG), :] for g in range(2)]
-        out_ref[n, 0] = jnp.concatenate(v, axis=-1).astype(BF)
+    write_out(inner)
 
     for_col(lambda c: m_xcol(c).wait_send())
 
@@ -542,15 +594,13 @@
         for h in range(2):
             m_xtop(h).wait_send()
 
-        @pl.loop(0, N)
-        def _(k):
+        for k in range(N):
             for m in (m_y1d, m_z1, m_y2d, m_z2, m_y3d):
                 m(k).wait_send()
 
     @pl.when(has_up)
     def _():
-        @pl.loop(0, N)
-        def _(k):
+        for k in range(N):
             for m in (m_y1u, m_z1u, m_y3u):
                 m(k).wait_send()
 
@@ -582,6 +632,7 @@
         vm(c1 + 2, IMG, L), vm(c2 + 2, IMG, LL), vm(c3 + 2, IMG, LL), vm(c3 + 2, IMG, LL), vm(c2 + 1, 2, IMG, L), vm(c2 + 1, 2, IMG, L), vm(c3 + 1, 2, IMG, L),
         pltpu.SemaphoreType.DMA((2,)), pltpu.SemaphoreType.DMA((15,)),
         pltpu.SemaphoreType.DMA((MESSAGES, N)), pltpu.SemaphoreType.DMA((MESSAGES, N)),
+        pltpu.SemaphoreType.REGULAR,
     ]
 
     def local(x_tile, *params):

time: 30.5 us -> 29.2 us (0.957)
  Pallas kernels: 29.7 us -> 28.3 us
    pallas_call x1, Pallas kernels: 29.7 us -> 28.3 us  [local(): pl.pallas_call(functools.partial(_body, row_count), out_shape=pltpu.VMEM(...]
where the time goes in v2:
time: 29.2 us; the launch traced here: 29.1 us
  Pallas kernels  28.3 us (97%)
  local copies, waits for them, and re-layouts  0.71 us (2%)
    pallas_call x1, Pallas kernels, local(): pl.pallas_call(functools.partial(_body, row_count), out_shape=pltpu.VMEM(...  28.3 us
    unnamed x1, local copies, waits for them, and re-layouts  0.71 us

profile of v2, /device:TPU:1, one launch (start us, length us, event | category | flops | bytes accessed | tf_op | source)
XLA Modules:
  0.0 29.1 jit_solution(1019352929696749431)
XLA Ops:
  0.0 28.3 %shard_map.154 = bf16[16,1,32,256]{3,2,1,0:T(8,128)(2,1)S(1)} custom-call(bf16[16,8,32,256]{3,2,1,0:T(8,128)(2,1)} %bitcast.7, bf16[3,3,32,64]{3,2,1,0:T(8,128)(2,1)} %refs_1_.1, f32[1,64]{1,0:T(1,128)} %bitcast.10, bf16[3,3,64,64]{3,2,1,0:T(8,128)(2,1)} %refs_3_.1, f32[1,64]{1,0:T(1,128)} %bitcast.11, bf16[32,64]{1,0:T(8,128)(2,1)} %refs_5_.1, ...), custom_call_target="tpu_custom_call" | custom-call | tf_op jit(solution)/shard_map/pallas_call | solution.py:642
  28.4 0.7 %copy.18 = bf16[16,1,32,256]{3,2,1,0:T(8,128)(2,1)} copy(bf16[16,1,32,256]{3,2,1,0:T(8,128)(2,1)S(1)} %shard_map.154) | data formatting | bytes 524288

commit v3 on v2

--- a/solution.py
+++ b/solution.py
@@ -18,17 +18,20 @@
 LO = slice(0, L)
 HI = slice(L, LL)
 IMG = 16
-N = 5
+SIZES = (5, 5, 5, 6, 7, 7)
+N = len(SIZES)
+EDGE = 3
 PAD = 12
 NEED = (11, 7)
 COLS = (140, 70, 35)
-M = tuple(p // N for p in COLS)
-MH = M[0] // 2
 STEP = 132
 TAPS = range(3)
 MIB = 1024 * 1024
 
-(X_TOP, X_COL, Y1_DOWN, Y1_UP, Z1_DOWN, Y2_DOWN, Z1_UP, Z2_DOWN, Y3_DOWN, Y3_UP, MESSAGES) = range(11)
+(X_TOP, DIAG, X_COL, Y1_DOWN, Y1_UP, Z1_DOWN, Y2_DOWN, Z1_UP, Z2_DOWN, Y3_DOWN, Y3_UP, MESSAGES) = range(12)
+SLOT = {X_TOP: 0, DIAG: 2, X_COL: 3, **{m: 4 + N * i for i, m in enumerate((Y1_DOWN, Y1_UP, Z1_DOWN, Y2_DOWN, Z1_UP))}}
+SLOT[Z2_DOWN], SLOT[Y3_UP] = SLOT[Y1_DOWN], SLOT[Y1_UP]
+SLOTS = 4 + 5 * N
 
 
 def _dot(a, b):
@@ -87,28 +90,42 @@
     def _():
         greet(down)
 
-    def x_copy(h):
-        return pltpu.make_async_copy(x_hbm.at[:, :, :, pl.ds(pl.multiple_of(h * L, L), L)], xv.at[h], xsem.at[h])
+    def x_copy(h, part):
+        rows = pl.ds(*((7, 1), (0, 4), (4, 3), (0, 7))[part])
+        return pltpu.make_async_copy(x_hbm.at[:, rows, :, pl.ds(pl.multiple_of(h * L, L), L)], xv.at[h, :, rows],
+                                     xsem.at[h, min(part, 1)])
 
     w_copies = [pltpu.make_async_copy(s, d, wsem.at[i]) for i, (s, d) in enumerate(
         ((wd1_h, wd1r), (bd1_h, bd1), (bc1_h, bc1), (bd2_h, bd2), (bc2_h, bc2), (bd3_h, bd3), (bc3_h, bc3),
          (wc1_h, wc1r), (wp1_h, wp1r), (wd2_h, wd2r), (wc2_h, wc2r), (wp2_h, wp2r),
          (wd3_h, wd3), (wc3_h, wc3), (wp3_h, wp3)))]
     first_copies, late_copies = w_copies[:7], w_copies[7:]
-    x_copy(inner).start()
+    x_copy(outer, 0).start()
+    x_copy(inner, 0).start()
+    for h in (inner, outer):
+        for part in (1, 2):
+            x_copy(h, part).start()
     for c in first_copies:
         c.start()
-    x_copy(outer).start()
+
+    def span(k, stage):
+        before, scale = sum(SIZES[:k]), COLS[stage - 1] // COLS[2]
+        first = before + col * (COLS[2] - SIZES[k] - 2 * before)
+        return scale * first, scale * SIZES[k]
 
     def remote(src, dst, msg, k, dev):
-        return pltpu.make_async_remote_copy(src_ref=src, dst_ref=dst, send_sem=ssem.at[msg, k], recv_sem=rsem.at[msg, k],
+        k = 0 if k is None else k
+        got = wsem.at[k] if msg == Y3_DOWN else rsem.at[SLOT[msg] + k]
+        return pltpu.make_async_remote_copy(src_ref=src, dst_ref=dst, send_sem=ssem.at[msg], recv_sem=got,
                                             device_id=dev, device_id_type=MESH)
 
     def m_xtop(h):
+        if h is None:
+            return remote(xtop, xtop, X_TOP, h, down)
         return remote(xv.at[h, :, 7], xtop.at[h], X_TOP, h, down)
 
     def m_diag():
-        return remote(sdiag, rdiag, X_TOP, 2, diag_down)
+        return remote(sdiag, rdiag, DIAG, 0, diag_down)
 
     own_edge = 1 + (L - PAD) * inner + PAD * col
     far_edge = 1 + L * col
@@ -123,41 +140,41 @@
             def _():
                 fn(c)
 
-    def chunk(k, size, need):
+    def chunk(k, stage, spare):
+        if k is None:
+            return pl.ds(1, COLS[stage - 1] - spare)
+        first, size = span(k, stage)
         if k == N - 1:
-            return pl.ds(1 + order(k) * size + (size - need) * col, need)
-        return pl.ds(1 + order(k) * size, size)
-
-    def plain(src, dst, msg, dev, size, need, src_lanes=None, dst_lanes=None):
+            return pl.ds(1 + first + spare * col, size - spare)
+        return pl.ds(1 + first, size)
+
+    def plain(src, dst, msg, dev, stage, spare, src_lanes=None, dst_lanes=None):
         def make(k):
-            s = chunk(k, size, need)
+            s = chunk(k, stage, spare)
             return remote(src.at[s] if src_lanes is None else src.at[s, :, src_lanes],
                           dst.at[s] if dst_lanes is None else dst.at[s, :, dst_lanes], msg, k, dev)
         return make
 
-    def order(k):
-        return k + col * (N - 1 - 2 * k)
-
     lanes_lo, lanes_hi = pl.ds(0, L), pl.ds(L, L)
     def packed(src, dst, msg, dev):
         def make(k):
-            s = pl.ds(order(k) * MH, MH)
+            s = pl.ds(0, COLS[1]) if k is None else pl.ds(*span(k, 2))
             return remote(src.at[s], dst.at[s], msg, k, dev)
         return make
 
     m_y1d = packed(sy1d, ry1d, Y1_DOWN, down)
     m_y1u = packed(sy1u, ry1u, Y1_UP, up)
     m_z1 = packed(sz1, rz1, Z1_DOWN, down)
-    m_y2d = plain(y2, yh2, Y2_DOWN, down, M[1], 12, lanes_hi, lanes_lo)
-    m_y3d = plain(y3, yt3, Y3_DOWN, down, M[2], 5)
-    m_y3u = plain(y3, yb3, Y3_UP, up, M[2], 5)
+    m_y2d = plain(y2, yh2, Y2_DOWN, down, 2, 2, lanes_hi, lanes_lo)
+    m_y3d = plain(y3, yt3, Y3_DOWN, down, 3, 2)
+    m_y3u = plain(y3, yb3, Y3_UP, up, 3, 2)
 
     def m_z1u(k):
-        s = chunk(k, MH, 13)
+        s = chunk(k, 2, 1)
         return remote(z1.at[s, :, :, lanes_lo], zb1.at[s], Z1_UP, k, up)
 
     def m_z2(k):
-        s = chunk(k, M[2], 6)
+        s = chunk(k, 3, 1)
         return remote(z2.at[s, :, :, lanes_hi], zh2.at[s], Z2_DOWN, k, down)
 
     def send(downs, ups, k):
@@ -192,10 +209,9 @@
     vertical = jnp.minimum(row, 1) + jnp.minimum(row_count - 1 - row, 1)
     pl.semaphore_wait(barrier, 1 + vertical)
 
-    x_copy(outer).wait()
-    x_copy(inner).wait()
-    send([m_xtop], [], outer)
-    send([m_xtop], [], inner)
+    for h in (outer, inner):
+        x_copy(h, 0).wait()
+        send([m_xtop], [], h)
     @pl.when(has_up)
     def _():
         pl.semaphore_signal(near_sem, inc=1, device_id=up, device_id_type=MESH)
@@ -291,11 +307,13 @@
         xh[pl.ds(1 + L * (1 - col), PAD)] = u.reshape(PAD, 2, IMG, L)
 
     border = (H - PAD) * inner
+    x_copy(inner, 3).wait()
     transpose_half(inner)
     gather_pairs(inner, border, PAD)
     for_col(lambda c: m_xcol(c).start())
     pack_diag()
     gather_pairs(inner, PAD * col, H - PAD)
+    x_copy(outer, 3).wait()
     transpose_half(outer)
     gather_pairs(outer, 0, H)
     pl.semaphore_wait(near_sem, vertical)
@@ -323,112 +341,114 @@
     def tiles(v, m):
         return v.reshape(m, IMG, v.shape[-1])
 
-    low = _lane((MH, IMG, L)) < H
-
     def pack(a, b):
-        return jnp.where(low, a, b).astype(BF)
-
-    m1, m2, m3 = M
-
-    def above1(j0):
-        a, b, c = pair_taps(xh, j0, m1)
+        return jnp.where(_lane(a.shape) < H, a, b).astype(BF)
+
+    def above1(j0, m):
+        a, b, c = pair_taps(xh, j0, m)
         ln = _lane(a.shape)
-        return tiles(_dot(jnp.where(ln < Q, a, jnp.where(ln < H, b, c)), wdh1[...]), m1)
+        return tiles(_dot(jnp.where(ln < Q, a, jnp.where(ln < H, b, c)), wdh1[...]), m)
 
     def store_top1(k, v):
+        j0, m = span(k, 1)
+        p = m // 2
         lo = _relu(v + bias[0, :, LO])
-        y1[pl.ds(1 + order(k) * m1, m1), :, LO] = lo.astype(BF)
-        sy1u[pl.ds(order(k) * MH, MH)] = pack(lo[:MH], _roll(lo[MH:], H))
+        y1[pl.ds(1 + j0, m), :, LO] = lo.astype(BF)
+        sy1u[pl.ds(*span(k, 2))] = pack(lo[:p], _roll(lo[p:], H))
 
     def down1(k, whole=False):
-        j0 = order(k) * m1
-        v = tiles(sum_dots(pair_taps(xt, j0, m1), lambda t: wd1[t]), m1)
+        j0, m = span(k, 1)
+        p = m // 2
+        v = tiles(sum_dots(pair_taps(xt, j0, m), lambda t: wd1[t]), m)
         if whole:
-            store_top1(k, v[:, :, LO] + above1(j0))
+            store_top1(k, v[:, :, LO] + above1(j0, m))
         else:
-            part1[pl.ds(j0, m1)] = v[:, :, LO]
+            part1[pl.ds(j0, m)] = v[:, :, LO]
         hi = _relu(v[:, :, HI] + bias[0, :, HI])
-        y1[pl.ds(1 + j0, m1), :, HI] = hi.astype(BF)
-        sy1d[pl.ds(order(k) * MH, MH)] = pack(_roll(hi[:MH], H), hi[MH:])
+        y1[pl.ds(1 + j0, m), :, HI] = hi.astype(BF)
+        sy1d[pl.ds(*span(k, 2))] = pack(_roll(hi[:p], H), hi[p:])
 
     def top1(k):
-        j0 = order(k) * m1
-        store_top1(k, above1(j0) + part1[pl.ds(j0, m1)])
+        j0, m = span(k, 1)
+        store_top1(k, above1(j0, m) + part1[pl.ds(j0, m)])
 
     def conv1(k):
-        j0 = order(k) * m1
-        v = sum_dots(taps(y1, j0, m1), lambda t: wc1[t]) + _dot(_flat(xt[pl.ds(j0 + 1, m1), 0]), wpp1[...])
-        acc1[pl.ds(j0, m1)] = tiles(v, m1) + bias[1]
+        j0, m = span(k, 1)
+        v = sum_dots(taps(y1, j0, m), lambda t: wc1[t]) + _dot(_flat(xt[pl.ds(j0 + 1, m), 0]), wpp1[...])
+        acc1[pl.ds(j0, m)] = tiles(v, m) + bias[1]
 
     def unpack1(k):
-        s = pl.ds(order(k) * MH, MH)
-        t, b = ry1d[s].astype(F32), ry1u[s].astype(F32)
-        yh1[pl.ds(1 + order(k) * m1, MH)] = pack(t, _roll(b, H))
-        yh1[pl.ds(1 + order(k) * m1 + MH, MH)] = pack(_roll(t, H), b)
+        s, p = span(k, 2)
+        j0 = span(k, 1)[0]
+        t, b = ry1d[pl.ds(s, p)].astype(F32), ry1u[pl.ds(s, p)].astype(F32)
+        yh1[pl.ds(1 + j0, p)] = pack(t, _roll(b, H))
+        yh1[pl.ds(1 + j0 + p, p)] = pack(_roll(t, H), b)
 
     def halo1(k):
-        j0 = order(k) * m1
-        v = tiles(sum_narrow(taps(yh1, j0, m1), lambda t: wch1[t]), m1)
-        v = _relu(v + acc1[pl.ds(j0, m1)])
-        z1[pl.ds(1 + order(k) * MH, MH)] = v.astype(BF).reshape(MH, 2, IMG, LL)
+        j0, m = span(k, 1)
+        s, p = span(k, 2)
+        v = tiles(sum_narrow(taps(yh1, j0, m), lambda t: wch1[t]), m)
+        v = _relu(v + acc1[pl.ds(j0, m)])
+        z1[pl.ds(1 + s, p)] = v.astype(BF).reshape(p, 2, IMG, LL)
         hi = v[:, :, HI]
-        sz1[pl.ds(order(k) * MH, MH)] = pack(_roll(hi[:MH], H), hi[MH:])
+        sz1[pl.ds(s, p)] = pack(_roll(hi[:p], H), hi[p:])
 
     def down2(k):
-        j0 = order(k) * m2
+        j0, m2 = span(k, 2)
         v = tiles(sum_dots(pair_taps(z1, j0, m2), lambda t: wd2[t]), m2)
         part2[pl.ds(j0, m2)] = v[:, :, LO]
         y2[pl.ds(1 + j0, m2), :, HI] = _relu(v[:, :, HI] + bias[2, :, HI]).astype(BF)
 
     def unpack2(k):
-        s = order(k) * MH
-        half = MH // 2
-        t = rz1[pl.ds(s, MH)].astype(F32)
+        s, p = span(k, 2)
+        half = p // 2
+        t = rz1[pl.ds(s, p)].astype(F32)
         u = _roll(t, H)
         zh1[pl.ds(1 + s, half)] = pack(t, u).reshape(half, 2, IMG, L)
         zh1[pl.ds(1 + s + half, half)] = pack(u, t).reshape(half, 2, IMG, L)
 
     def top2(k):
-        j0 = order(k) * m2
+        j0, m2 = span(k, 2)
         a, b, c = pair_taps(zh1, j0, m2)
         t = jnp.concatenate([jnp.where(_lane(a.shape) < H, a, b), c], axis=-1)
         v = tiles(_dot(t, wdh2[...]), m2) + part2[pl.ds(j0, m2)]
         y2[pl.ds(1 + j0, m2), :, LO] = _relu(v + bias[2, :, LO]).astype(BF)
 
     def bottom2(k):
-        j0 = order(k) * m2
+        j0, m2 = span(k, 2)
         own, below = pair_taps(z1, j0, m2), pair_taps(zb1, j0, m2)
         lhs = [jnp.concatenate([a[:, HI], b], axis=-1) for a, b in zip(own, below)]
         v = _relu(tiles(sum_dots(lhs, lambda t: wdb2[t]), m2) + bias[2, :, LO])
         yh2[pl.ds(1 + j0, m2), :, HI] = jnp.where(has_down, v, 0.0).astype(BF)
 
     def conv2(k):
-        j0 = order(k) * m2
+        j0, m2 = span(k, 2)
         v = sum_dots(taps(y2, j0, m2), lambda t: wc2[t]) + _dot(_flat(z1[pl.ds(j0 + 1, m2), 0]), wpp2[...])
         acc2[pl.ds(j0, m2)] = tiles(v, m2) + bias[3]
 
     def halo2(k):
-        j0 = order(k) * m2
+        j0, m2 = span(k, 2)
         v = tiles(sum_dots(taps(yh2, j0, m2), lambda t: wch2[t]), m2) + acc2[pl.ds(j0, m2)]
-        z2[pl.ds(1 + order(k) * m3, m3)] = _relu(v).astype(BF).reshape(m3, 2, IMG, LL)
+        s, p = span(k, 3)
+        z2[pl.ds(1 + s, p)] = _relu(v).astype(BF).reshape(p, 2, IMG, LL)
 
     def down3(k):
-        j0 = order(k) * m3
+        j0, m3 = span(k, 3)
         v = sum_dots(pair_taps(z2, j0, m3), lambda t: wd3[1:, t].reshape(LL, LL))
         part3[pl.ds(j0, m3)] = tiles(v, m3) + bias[4]
 
     def top3(k):
-        j0 = order(k) * m3
+        j0, m3 = span(k, 3)
         v = tiles(sum_narrow(pair_taps(zh2, j0, m3), lambda t: wd3[0, t]), m3) + part3[pl.ds(j0, m3)]
         y3[pl.ds(1 + j0, m3)] = _relu(v).astype(BF)
 
     def conv3(k):
-        j0 = order(k) * m3
+        j0, m3 = span(k, 3)
         v = sum_dots(taps(y3, j0, m3), lambda t: wc3[1, t]) + _dot(_flat(z2[pl.ds(j0 + 1, m3), 0, :, LO]), wp3[...])
         acc3[pl.ds(j0, m3)] = tiles(v, m3) + bias[5]
 
     def halo3(k):
-        j0 = order(k) * m3
+        j0, m3 = span(k, 3)
         v = sum_dots(taps(yt3, j0, m3), lambda t: wc3[0, t]) + sum_dots(taps(yb3, j0, m3), lambda t: wc3[2, t])
         v = _relu(tiles(v, m3) + acc3[pl.ds(j0, m3)])
         r = pl.ds(pl.multiple_of(j0 * IMG, IMG), m3 * IMG)
@@ -466,17 +486,16 @@
 
     recv([m_xtop], [], outer)
     transpose_top(outer)
-    top1(0)
-    send([], [m_y1u], 0)
-    top1(1)
-    send([], [m_y1u], 1)
+    for k in range(EDGE):
+        top1(k)
+        send([], [m_y1u], k)
 
     recv([m_xtop], [], inner)
     transpose_top(inner)
-    top1(2)
-    top1(3)
-    send([], [m_y1u], 2)
-    send([], [m_y1u], 3)
+    for k in range(EDGE, last):
+        top1(k)
+    for k in range(EDGE, last):
+        send([], [m_y1u], k)
     conv1(0)
 
     def border1():
@@ -510,11 +529,11 @@
         if k < last:
             conv1(k + 1)
         send([m_z1], [m_z1u], k)
-    for k in range(3):
+    for k in range(N - 2):
         send([m_y2d], [], k)
-    down2(3)
+    down2(last - 1)
     down2(last)
-    send([m_y2d], [], 3)
+    send([m_y2d], [], last - 1)
     send([m_y2d], [], last)
 
     def above2(k):
@@ -535,7 +554,7 @@
         if k + 2 < N:
             above2(k + 2)
         else:
-            conv2(3)
+            conv2(last - 1)
             conv2(last)
         recv([], [m_z1u], k + 1)
         bottom2(k)
@@ -543,27 +562,28 @@
             bottom2(last)
         if k:
             wait_next([m_y2d], [], k - 1)
-            if k == last - 1:
-                down3(0)
+            if k >= 3:
+                down3(k - 3)
             halo2(k - 1)
             send([m_z2], [], k - 1)
     recv([m_y2d], [], last)
-    down3(1)
-    halo2(3)
+    down3(last - 3)
+    halo2(last - 1)
     halo2(last)
-    send([m_z2], [], 3)
+    send([m_z2], [], last - 1)
     send([m_z2], [], last)
 
     recv([m_z2], [], 0)
-    for k in range(3):
+    for k in range(last - 1):
         recv([m_z2], [], k + 1)
         top3(k)
-        down3(k + 2)
+        if k < 3:
+            down3(last - 2 + k)
         send([m_y3d], [m_y3u], k)
     recv([m_z2], [], last)
-    top3(3)
+    top3(last - 1)
     top3(last)
-    send([m_y3d], [m_y3u], 3)
+    send([m_y3d], [m_y3u], last - 1)
     send([m_y3d], [m_y3u], last)
     for k in range(N):
         conv3(k)
@@ -576,33 +596,36 @@
             v = [zo[g, pl.ds(PAD * 4 * col + half * IMG * h + n, half, stride=IMG), :] for g in range(2)]
             out_ref[n, 0, pl.ds(lo, half)] = jnp.concatenate(v, axis=-1).astype(BF)
 
-    for k in range(3):
+    def sent(downs, ups):
+        @pl.when(has_down)
+        def _():
+            for m in downs:
+                m(None).wait_send()
+
+        @pl.when(has_up)
+        def _():
+            for m in ups:
+                m(None).wait_send()
+
+    for_col(lambda c: m_xcol(c).wait_send())
+
+    @pl.when(has_down)
+    def _():
+        m_diag().wait_send()
+        m_xtop(None).wait_send()
+
+    sent([m_y1d, m_z1, m_y2d, m_z2], [m_y1u, m_z1u])
+
+    for k in range(last - 1):
         wait_next([m_y3d], [m_y3u], k)
-    for k in range(3):
+    for k in range(last - 1):
         halo3(k)
     write_out(outer)
+    sent([m_y3d], [m_y3u])
     recv([m_y3d], [m_y3u], last)
-    halo3(3)
+    halo3(last - 1)
     halo3(last)
     write_out(inner)
-
-    for_col(lambda c: m_xcol(c).wait_send())
-
-    @pl.when(has_down)
-    def _():
-        m_diag().wait_send()
-        for h in range(2):
-            m_xtop(h).wait_send()
-
-        for k in range(N):
-            for m in (m_y1d, m_z1, m_y2d, m_z2, m_y3d):
-                m(k).wait_send()
-
-    @pl.when(has_up)
-    def _():
-        for k in range(N):
-            for m in (m_y1u, m_z1u, m_y3u):
-                m(k).wait_send()
 
 
 def solution(mesh):
@@ -630,8 +653,8 @@
         vm(2, c3 * IMG, L, dtype=F32),
         *[packed] * 6,
         vm(c1 + 2, IMG, L), vm(c2 + 2, IMG, LL), vm(c3 + 2, IMG, LL), vm(c3 + 2, IMG, LL), vm(c2 + 1, 2, IMG, L), vm(c2 + 1, 2, IMG, L), vm(c3 + 1, 2, IMG, L),
-        pltpu.SemaphoreType.DMA((2,)), pltpu.SemaphoreType.DMA((15,)),
-        pltpu.SemaphoreType.DMA((MESSAGES, N)), pltpu.SemaphoreType.DMA((MESSAGES, N)),
+        pltpu.SemaphoreType.DMA((2, 2)), pltpu.SemaphoreType.DMA((15,)),
+        pltpu.SemaphoreType.DMA((MESSAGES,)), pltpu.SemaphoreType.DMA((SLOTS,)),
         pltpu.SemaphoreType.REGULAR,
     ]
 

time: 29.2 us -> 28.1 us (0.962)
  Pallas kernels: 28.3 us -> 27.3 us
    pallas_call x1, Pallas kernels: 28.3 us -> 27.3 us  [local(): pl.pallas_call(functools.partial(_body, row_count), out_shape=pltpu.VMEM(...]
where the time goes in v3:
time: 28.1 us; the launch traced here: 28 us
  Pallas kernels  27.3 us (97%)
  local copies, waits for them, and re-layouts  0.71 us (3%)
    pallas_call x1, Pallas kernels, local(): pl.pallas_call(functools.partial(_body, row_count), out_shape=pltpu.VMEM(...  27.3 us
    unnamed x1, local copies, waits for them, and re-layouts  0.71 us

profile of v3, /device:TPU:1, one launch (start us, length us, event | category | flops | bytes accessed | tf_op | source)
XLA Modules:
  0.0 28.0 jit_solution(13179511518330866803)
XLA Ops:
  0.0 27.3 %shard_map.154 = bf16[16,1,32,256]{3,2,1,0:T(8,128)(2,1)S(1)} custom-call(bf16[16,8,32,256]{3,2,1,0:T(8,128)(2,1)} %bitcast.7, bf16[3,3,32,64]{3,2,1,0:T(8,128)(2,1)} %refs_1_.1, f32[1,64]{1,0:T(1,128)} %bitcast.10, bf16[3,3,64,64]{3,2,1,0:T(8,128)(2,1)} %refs_3_.1, f32[1,64]{1,0:T(1,128)} %bitcast.11, bf16[32,64]{1,0:T(8,128)(2,1)} %refs_5_.1, ...), custom_call_target="tpu_custom_call" | custom-call | tf_op jit(solution)/shard_map/pallas_call | solution.py:665
  27.3 0.7 %copy.18 = bf16[16,1,32,256]{3,2,1,0:T(8,128)(2,1)} copy(bf16[16,1,32,256]{3,2,1,0:T(8,128)(2,1)S(1)} %shard_map.154) | data formatting | bytes 524288

commit v4 on v3

--- a/solution.py
+++ b/solution.py
@@ -29,9 +29,19 @@
 MIB = 1024 * 1024
 
 (X_TOP, DIAG, X_COL, Y1_DOWN, Y1_UP, Z1_DOWN, Y2_DOWN, Z1_UP, Z2_DOWN, Y3_DOWN, Y3_UP, MESSAGES) = range(12)
-SLOT = {X_TOP: 0, DIAG: 2, X_COL: 3, **{m: 4 + N * i for i, m in enumerate((Y1_DOWN, Y1_UP, Z1_DOWN, Y2_DOWN, Z1_UP))}}
+SLOT = {X_TOP: (0, 1), DIAG: (2,), X_COL: (3,)}
+WEIGHTS = 15
+OWN = 4 + WEIGHTS
+for i, m in enumerate((Y1_DOWN, Y1_UP, Z1_UP)):
+    SLOT[m] = tuple(range(OWN + N * i, OWN + N * i + N))
 SLOT[Z2_DOWN], SLOT[Y3_UP] = SLOT[Y1_DOWN], SLOT[Y1_UP]
-SLOTS = 4 + 5 * N
+SLOT[Z1_DOWN], SLOT[Y2_DOWN] = tuple(range(4, 4 + N)), tuple(range(4 + N, 4 + 2 * N))
+SLOT[Y3_DOWN] = tuple(range(4 + 2 * N, OWN)) + SLOT[X_TOP] + SLOT[DIAG]
+OUT = {X_TOP: 0, DIAG: 1, X_COL: 2, **{m: 3 for m in (Y1_DOWN, Z1_DOWN, Y2_DOWN, Z2_DOWN, Y3_DOWN)},
+       **{m: 4 for m in (Y1_UP, Z1_UP, Y3_UP)}}
+ROWS_DOWN = 8 * (2 * COLS[1] + COLS[1] - 2 + 2 * (COLS[2] - 1) + 2 * (COLS[2] - 2))
+ROWS_UP = 8 * (COLS[1] + 2 * (COLS[1] - 1) + 2 * (COLS[2] - 2))
+SLOTS = OWN + 3 * N
 
 
 def _dot(a, b):
@@ -63,7 +73,7 @@
      part1, part2, part3, acc1, acc2, acc3, y1, y2, y3, z1, z2, zo,
      sy1d, sy1u, sz1, ry1d, ry1u, rz1,
      yh1, yh2, yt3, yb3, zh1, zb1, zh2,
-     xsem, wsem, ssem, rsem, near_sem) = refs
+     xsem, ssem, rsem, near_sem) = refs
 
     row = lax.axis_index("row")
     col = lax.axis_index("col")
@@ -95,7 +105,7 @@
         return pltpu.make_async_copy(x_hbm.at[:, rows, :, pl.ds(pl.multiple_of(h * L, L), L)], xv.at[h, :, rows],
                                      xsem.at[h, min(part, 1)])
 
-    w_copies = [pltpu.make_async_copy(s, d, wsem.at[i]) for i, (s, d) in enumerate(
+    w_copies = [pltpu.make_async_copy(s, d, rsem.at[4 + i]) for i, (s, d) in enumerate(
         ((wd1_h, wd1r), (bd1_h, bd1), (bc1_h, bc1), (bd2_h, bd2), (bc2_h, bc2), (bd3_h, bd3), (bc3_h, bc3),
          (wc1_h, wc1r), (wp1_h, wp1r), (wd2_h, wd2r), (wc2_h, wc2r), (wp2_h, wp2r),
          (wd3_h, wd3), (wc3_h, wc3), (wp3_h, wp3)))]
@@ -114,14 +124,13 @@
         return scale * first, scale * SIZES[k]
 
     def remote(src, dst, msg, k, dev):
-        k = 0 if k is None else k
-        got = wsem.at[k] if msg == Y3_DOWN else rsem.at[SLOT[msg] + k]
-        return pltpu.make_async_remote_copy(src_ref=src, dst_ref=dst, send_sem=ssem.at[msg], recv_sem=got,
+        slot = SLOT[msg][k] if isinstance(k, int) else k
+        return pltpu.make_async_remote_copy(src_ref=src, dst_ref=dst, send_sem=ssem.at[OUT[msg]], recv_sem=rsem.at[slot],
                                             device_id=dev, device_id_type=MESH)
 
     def m_xtop(h):
         if h is None:
-            return remote(xtop, xtop, X_TOP, h, down)
+            return remote(xtop, xtop, X_TOP, 0, down)
         return remote(xv.at[h, :, 7], xtop.at[h], X_TOP, h, down)
 
     def m_diag():
@@ -141,8 +150,6 @@
                 fn(c)
 
     def chunk(k, stage, spare):
-        if k is None:
-            return pl.ds(1, COLS[stage - 1] - spare)
         first, size = span(k, stage)
         if k == N - 1:
             return pl.ds(1 + first + spare * col, size - spare)
@@ -158,7 +165,7 @@
     lanes_lo, lanes_hi = pl.ds(0, L), pl.ds(L, L)
     def packed(src, dst, msg, dev):
         def make(k):
-            s = pl.ds(0, COLS[1]) if k is None else pl.ds(*span(k, 2))
+            s = pl.ds(*span(k, 2))
             return remote(src.at[s], dst.at[s], msg, k, dev)
         return make
 
@@ -596,17 +603,6 @@
             v = [zo[g, pl.ds(PAD * 4 * col + half * IMG * h + n, half, stride=IMG), :] for g in range(2)]
             out_ref[n, 0, pl.ds(lo, half)] = jnp.concatenate(v, axis=-1).astype(BF)
 
-    def sent(downs, ups):
-        @pl.when(has_down)
-        def _():
-            for m in downs:
-                m(None).wait_send()
-
-        @pl.when(has_up)
-        def _():
-            for m in ups:
-                m(None).wait_send()
-
     for_col(lambda c: m_xcol(c).wait_send())
 
     @pl.when(has_down)
@@ -614,14 +610,25 @@
         m_diag().wait_send()
         m_xtop(None).wait_send()
 
-    sent([m_y1d, m_z1, m_y2d, m_z2], [m_y1u, m_z1u])
 
     for k in range(last - 1):
         wait_next([m_y3d], [m_y3u], k)
     for k in range(last - 1):
         halo3(k)
     write_out(outer)
-    sent([m_y3d], [m_y3u])
+
+    def all_sent(msg, rows, dev):
+        ref = fs.at[:, pl.ds(0, rows // 2)]
+        remote(ref, ref, msg, 0, dev).wait_send()
+
+    @pl.when(has_down)
+    def _():
+        all_sent(Y1_DOWN, ROWS_DOWN, down)
+
+    @pl.when(has_up)
+    def _():
+        all_sent(Y1_UP, ROWS_UP, up)
+
     recv([m_y3d], [m_y3u], last)
     halo3(last - 1)
     halo3(last)
@@ -653,8 +660,7 @@
         vm(2, c3 * IMG, L, dtype=F32),
         *[packed] * 6,
         vm(c1 + 2, IMG, L), vm(c2 + 2, IMG, LL), vm(c3 + 2, IMG, LL), vm(c3 + 2, IMG, LL), vm(c2 + 1, 2, IMG, L), vm(c2 + 1, 2, IMG, L), vm(c3 + 1, 2, IMG, L),
-        pltpu.SemaphoreType.DMA((2, 2)), pltpu.SemaphoreType.DMA((15,)),
-        pltpu.SemaphoreType.DMA((MESSAGES,)), pltpu.SemaphoreType.DMA((SLOTS,)),
+        pltpu.SemaphoreType.DMA((2, 2)), pltpu.SemaphoreType.DMA((5,)), pltpu.SemaphoreType.DMA((SLOTS,)),
         pltpu.SemaphoreType.REGULAR,
     ]
 

time: 28.1 us -> 27.9 us (level)
  no operation moved by 1% of the time
where the time goes in v4:
time: 27.9 us; the launch traced here: 27.8 us
  Pallas kernels  27.1 us (97%)
  local copies, waits for them, and re-layouts  0.71 us (3%)
    pallas_call x1, Pallas kernels, local(): pl.pallas_call(functools.partial(_body, row_count), out_shape=pltpu.VMEM(...  27.1 us
    unnamed x1, local copies, waits for them, and re-layouts  0.71 us

profile of v4, /device:TPU:1, one launch (start us, length us, event | category | flops | bytes accessed | tf_op | source)
XLA Modules:
  0.0 27.8 jit_solution(4020214989337138550)
XLA Ops:
  0.0 27.1 %shard_map.154 = bf16[16,1,32,256]{3,2,1,0:T(8,128)(2,1)S(1)} custom-call(bf16[16,8,32,256]{3,2,1,0:T(8,128)(2,1)} %bitcast.7, bf16[3,3,32,64]{3,2,1,0:T(8,128)(2,1)} %refs_1_.1, f32[1,64]{1,0:T(1,128)} %bitcast.10, bf16[3,3,64,64]{3,2,1,0:T(8,128)(2,1)} %refs_3_.1, f32[1,64]{1,0:T(1,128)} %bitcast.11, bf16[32,64]{1,0:T(8,128)(2,1)} %refs_5_.1, ...), custom_call_target="tpu_custom_call" | custom-call | tf_op jit(solution)/shard_map/pallas_call | solution.py:671
  27.1 0.7 %copy.18 = bf16[16,1,32,256]{3,2,1,0:T(8,128)(2,1)} copy(bf16[16,1,32,256]{3,2,1,0:T(8,128)(2,1)S(1)} %shard_map.154) | data formatting | bytes 524288

commit v5 on v4

--- a/solution.py
+++ b/solution.py
@@ -554,6 +554,18 @@
             conv2(k - 2)
         top2(k)
 
+    def recv_left(m, k):
+        if k == 0:
+            recv([m], [], 0)
+        else:
+            @pl.when(jnp.logical_and(has_up, col == 0))
+            def _():
+                m(k).wait_recv()
+        if k < last:
+            @pl.when(jnp.logical_and(has_up, col == 1))
+            def _():
+                m(k + 1).wait_recv()
+
     above2(0)
     above2(1)
     recv([], [m_z1u], 0)
@@ -563,6 +575,10 @@
         else:
             conv2(last - 1)
             conv2(last)
+        if k == last - 1:
+            recv_left(m_z2, 0)
+            top3(0)
+            send([m_y3d], [m_y3u], 0)
         recv([], [m_z1u], k + 1)
         bottom2(k)
         if k == last - 1:
@@ -580,18 +596,12 @@
     send([m_z2], [], last - 1)
     send([m_z2], [], last)
 
-    recv([m_z2], [], 0)
-    for k in range(last - 1):
-        recv([m_z2], [], k + 1)
+    for k in range(1, N):
+        recv_left(m_z2, k)
         top3(k)
-        if k < 3:
-            down3(last - 2 + k)
+        if k < 4:
+            down3(last - 3 + k)
         send([m_y3d], [m_y3u], k)
-    recv([m_z2], [], last)
-    top3(last - 1)
-    top3(last)
-    send([m_y3d], [m_y3u], last - 1)
-    send([m_y3d], [m_y3u], last)
     for k in range(N):
         conv3(k)
 
@@ -613,7 +623,6 @@
 
     for k in range(last - 1):
         wait_next([m_y3d], [m_y3u], k)
-    for k in range(last - 1):
         halo3(k)
     write_out(outer)
 

time: 27.9 us -> 27.3 us (0.978)
  Pallas kernels: 27.1 us -> 26.4 us
    pallas_call x1, Pallas kernels: 27.1 us -> 26.4 us  [local(): pl.pallas_call(functools.partial(_body, row_count), out_shape=pltpu.VMEM(...]
where the time goes in v5:
time: 27.3 us; the launch traced here: 27.1 us
  Pallas kernels  26.4 us (97%)
  local copies, waits for them, and re-layouts  0.71 us (3%)
    pallas_call x1, Pallas kernels, local(): pl.pallas_call(functools.partial(_body, row_count), out_shape=pltpu.VMEM(...  26.4 us
    unnamed x1, local copies, waits for them, and re-layouts  0.71 us

profile of v5, /device:TPU:1, one launch (start us, length us, event | category | flops | bytes accessed | tf_op | source)
XLA Modules:
  0.0 27.1 jit_solution(1574770386470317282)
XLA Ops:
  0.0 26.4 %shard_map.154 = bf16[16,1,32,256]{3,2,1,0:T(8,128)(2,1)S(1)} custom-call(bf16[16,8,32,256]{3,2,1,0:T(8,128)(2,1)} %bitcast.7, bf16[3,3,32,64]{3,2,1,0:T(8,128)(2,1)} %refs_1_.1, f32[1,64]{1,0:T(1,128)} %bitcast.10, bf16[3,3,64,64]{3,2,1,0:T(8,128)(2,1)} %refs_3_.1, f32[1,64]{1,0:T(1,128)} %bitcast.11, bf16[32,64]{1,0:T(8,128)(2,1)} %refs_5_.1, ...), custom_call_target="tpu_custom_call" | custom-call | tf_op jit(solution)/shard_map/pallas_call | solution.py:680
  26.4 0.7 %copy.18 = bf16[16,1,32,256]{3,2,1,0:T(8,128)(2,1)} copy(bf16[16,1,32,256]{3,2,1,0:T(8,128)(2,1)S(1)} %shard_map.154) | data formatting | bytes 524288

commit v6 on v5

--- a/solution.py
+++ b/solution.py
@@ -454,10 +454,15 @@
         v = sum_dots(taps(y3, j0, m3), lambda t: wc3[1, t]) + _dot(_flat(z2[pl.ds(j0 + 1, m3), 0, :, LO]), wp3[...])
         acc3[pl.ds(j0, m3)] = tiles(v, m3) + bias[5]
 
-    def halo3(k):
+    def add3(k, rows, kh):
         j0, m3 = span(k, 3)
-        v = sum_dots(taps(yt3, j0, m3), lambda t: wc3[0, t]) + sum_dots(taps(yb3, j0, m3), lambda t: wc3[2, t])
-        v = _relu(tiles(v, m3) + acc3[pl.ds(j0, m3)])
+        s = pl.ds(j0, m3)
+        acc3[s] = acc3[s] + tiles(sum_dots(taps(rows, j0, m3), lambda t: wc3[kh, t]), m3)
+
+    def halo3(k, rows, kh):
+        j0, m3 = span(k, 3)
+        v = tiles(sum_dots(taps(rows, j0, m3), lambda t: wc3[kh, t]), m3)
+        v = _relu(v + acc3[pl.ds(j0, m3)])
         r = pl.ds(pl.multiple_of(j0 * IMG, IMG), m3 * IMG)
         zo[0, r] = _flat(v[:, :, LO])
         zo[1, r] = _flat(v[:, :, HI])
@@ -620,16 +625,39 @@
         m_diag().wait_send()
         m_xtop(None).wait_send()
 
-
-    for k in range(last - 1):
-        wait_next([m_y3d], [m_y3u], k)
-        halo3(k)
-    write_out(outer)
-
     def all_sent(msg, rows, dev):
         ref = fs.at[:, pl.ds(0, rows // 2)]
         remote(ref, ref, msg, 0, dev).wait_send()
 
+    def finish(near, far):
+        near_recv, near_rows, near_kh = near
+        far_recv, far_rows, far_kh = far
+        for k in range(N):
+            near_recv(k)
+        for k in range(N):
+            add3(k, near_rows, near_kh)
+        far_recv(0)
+        for k in range(last - 1):
+            far_recv(k + 1)
+            halo3(k, far_rows, far_kh)
+        write_out(outer)
+        far_recv(last)
+        halo3(last - 1, far_rows, far_kh)
+        halo3(last, far_rows, far_kh)
+        write_out(inner)
+
+    above = (lambda k: recv([m_y3d], [], k), yt3, 0)
+    below = (lambda k: recv([], [m_y3u], k), yb3, 2)
+    near_below = lax.rem(row, 2) == 0
+
+    @pl.when(near_below)
+    def _():
+        finish(below, above)
+
+    @pl.when(jnp.logical_not(near_below))
+    def _():
+        finish(above, below)
+
     @pl.when(has_down)
     def _():
         all_sent(Y1_DOWN, ROWS_DOWN, down)
@@ -637,11 +665,6 @@
     @pl.when(has_up)
     def _():
         all_sent(Y1_UP, ROWS_UP, up)
-
-    recv([m_y3d], [m_y3u], last)
-    halo3(last - 1)
-    halo3(last)
-    write_out(inner)
 
 
 def solution(mesh):

time: 27.3 us -> 27.2 us (level)
  no operation moved by 1% of the time
where the time goes in v6:
time: 27.2 us; the launch traced here: 27 us
  Pallas kernels  26.3 us (97%)
  local copies, waits for them, and re-layouts  0.71 us (3%)
    pallas_call x1, Pallas kernels, local(): pl.pallas_call(functools.partial(_body, row_count), out_shape=pltpu.VMEM(...  26.3 us
    unnamed x1, local copies, waits for them, and re-layouts  0.71 us

profile of v6, /device:TPU:1, one launch (start us, length us, event | category | flops | bytes accessed | tf_op | source)
XLA Modules:
  0.0 27.0 jit_solution(16604739558491844579)
XLA Ops:
  0.0 26.3 %shard_map.154 = bf16[16,1,32,256]{3,2,1,0:T(8,128)(2,1)S(1)} custom-call(bf16[16,8,32,256]{3,2,1,0:T(8,128)(2,1)} %bitcast.7, bf16[3,3,32,64]{3,2,1,0:T(8,128)(2,1)} %refs_1_.1, f32[1,64]{1,0:T(1,128)} %bitcast.10, bf16[3,3,64,64]{3,2,1,0:T(8,128)(2,1)} %refs_3_.1, f32[1,64]{1,0:T(1,128)} %bitcast.11, bf16[32,64]{1,0:T(8,128)(2,1)} %refs_5_.1, ...), custom_call_target="tpu_custom_call" | custom-call | tf_op jit(solution)/shard_map/pallas_call | solution.py:703
  26.3 0.7 %copy.18 = bf16[16,1,32,256]{3,2,1,0:T(8,128)(2,1)} copy(bf16[16,1,32,256]{3,2,1,0:T(8,128)(2,1)S(1)} %shard_map.154) | data formatting | bytes 524288
